TPU v7x, 128 devices: a whole 4x4x4 slice. The times are simulated.
128 devices in a mesh: dp: 8 (over z, core), expert: 16 (over y, x).
Axes of the slice: x: 4, y: 4, z: 4, core: 2. Of those that a mesh axis runs over, the one named last changes fastest.
Arguments:
- frames: bfloat16 [16384, 1024], P(('dp', 'expert')), may hold values from -6 to 6
- norm_gain: float32 [1024], replicated, may hold values from 0.5 to 1.5
- norm_bias: float32 [1024], replicated, may hold values from -3 to 3
- routes: int32 [16384, 2], P(('dp', 'expert')), may hold values from 0 to 31, all different within a row; in each aligned block of 128 rows (0 to 127, 128 to 255, ...) at most 16 rows name the same one
- gate_codes: int32 [16384, 2], P(('dp', 'expert')), may hold values from 1 to 255
- limits: int32 [32], replicated, may hold values from 8 to 16
- up_weight: bfloat16 [128, 1024, 1024], P(('dp', 'expert')), may hold values from -0.1875 to 0.1875
- up_bias: float32 [128, 1024], P(('dp', 'expert')), may hold values from -3 to 3
- down_weight: bfloat16 [128, 1024, 1024], P(('dp', 'expert')), may hold values from -0.09375 to 0.09375
- down_bias: float32 [32, 1024], replicated, may hold values from -2 to 2
Outputs:
- mixed: bfloat16 [16384, 1024], P(('dp', 'expert'))
- load: int32 [32], replicated
Inputs may be any that keep to these rules, and one draw needn't show every extreme that they name: `routes`: in each aligned block of 128 rows (the rows of one device) no expert is named by more than 16 rows, and some block has an expert named by exactly 16 rows; the two entries of a row differ.
All inputs are finite; a program needn't handle non-finite values.
Results may differ from a plain program's by a relative error of at most 0.0051.
Values may be sent and summed in bfloat16 or wider, within the bound.
A program may use at most 64 MiB of HBM per device.

v0:
```python
import jax
import jax.numpy as jnp
from jax import lax
from jax.sharding import Mesh
from jax.sharding import PartitionSpec as P

DP = ("dp_0", "dp_1")
EXPERT = ("expert_0", "expert_1")
DP_EXPERT = ("dp_0", "dp_1", "expert_0", "expert_1")


epsilon = 1e-05


def over_axes(value, axes):
    for axis in axes:
        value = lax.psum(value, axis)
    return value


def layer_norm(frames, norm_gain, norm_bias):
    values = frames.astype(jnp.float32)
    center = jnp.mean(values, axis=-1, keepdims=True)
    shifted = values - center
    spread = jnp.mean(shifted * shifted, axis=-1, keepdims=True)
    return (shifted * lax.rsqrt(spread + epsilon) * norm_gain + norm_bias).astype(jnp.bfloat16)


def place_slots(routes_block, limits, expert_total, capacity):
    flat_routes = routes_block.reshape(-1)
    expert_ids = jnp.arange(expert_total, dtype=jnp.int32)
    expert_hits = (flat_routes[:, None] == expert_ids[None, :]).astype(jnp.int32)
    earlier = jnp.cumsum(expert_hits, axis=0) - expert_hits
    slot_rank = jnp.sum(earlier * expert_hits, axis=1)
    slot_bound = jnp.sum(expert_hits * limits[None, :], axis=1)
    kept_mask = (slot_rank < slot_bound).astype(jnp.int32)
    slot_index = jnp.minimum(flat_routes * capacity + slot_rank, expert_total * capacity - 1)
    slot_ids = jnp.arange(expert_total * capacity, dtype=jnp.int32)
    matches = (slot_index[None, :] == slot_ids[:, None]).astype(jnp.int32) * kept_mask[None, :]
    frame_ids = jnp.arange(flat_routes.shape[0], dtype=jnp.int32) // 2
    source_frame = jnp.sum(matches * frame_ids[None, :], axis=1)
    filled = jnp.sum(matches, axis=1)
    expert_loads = jnp.sum(expert_hits * kept_mask[:, None], axis=0)
    return (slot_index, kept_mask, source_frame, filled, expert_loads)


def fill_slots(normed_block, source_frame, filled):
    slot_rows = jnp.take(normed_block, source_frame, axis=0)
    return slot_rows * filled[:, None].astype(jnp.bfloat16)


def combine(frames_block, returned, slot_index, kept_mask, gate_block):
    code_values = gate_block.astype(jnp.float32)
    shares = code_values / jnp.sum(code_values, axis=1, keepdims=True)
    weights = shares.reshape(-1) * kept_mask.astype(jnp.float32)
    picked = jnp.take(returned, slot_index, axis=0).astype(jnp.float32)
    weighted = (picked * weights[:, None]).reshape(frames_block.shape[0], 2, frames_block.shape[1])
    return (frames_block.astype(jnp.float32) + jnp.sum(weighted, axis=1)).astype(jnp.bfloat16)


def per_device(
    frames,
    norm_gain,
    norm_bias,
    routes,
    gate_codes,
    limits,
    up_weight,
    up_bias,
    down_weight,
    down_bias,
):
    owners = lax.axis_size(DP)
    holders = lax.axis_size(EXPERT)
    expert_total = down_bias.shape[0]
    row_experts = expert_total // owners
    groups = holders // row_experts
    frame_count = frames.shape[0]
    model_width = frames.shape[1]
    capacity = 4 * frame_count // expert_total
    normed = layer_norm(frames, norm_gain, norm_bias)
    slot_index, kept_mask, source_frame, filled, expert_loads = place_slots(
        routes, limits, expert_total, capacity
    )
    outgoing = fill_slots(normed, source_frame, filled)
    load_total = over_axes(expert_loads, DP_EXPERT)
    copies = jnp.repeat(
        outgoing.reshape(owners, row_experts, capacity, model_width), groups, axis=1
    )
    incoming = lax.all_to_all(
        copies.reshape(owners * holders * capacity, model_width),
        DP_EXPERT,
        split_axis=0,
        concat_axis=0,
        tiled=True,
    )
    preact = (
        jnp.dot(incoming, up_weight[0], preferred_element_type=jnp.float32) + up_bias[0][None, :]
    )
    hidden = jax.nn.gelu(preact, approximate=False).astype(jnp.bfloat16)
    partial_out = jnp.dot(hidden, down_weight[0], preferred_element_type=jnp.float32).astype(
        jnp.bfloat16
    )
    back = lax.all_to_all(partial_out, DP_EXPERT, split_axis=0, concat_axis=0, tiled=True)
    summed = jnp.sum(
        back.reshape(owners, row_experts, groups, capacity, model_width).astype(jnp.float32), axis=2
    )
    returned = (summed + down_bias.reshape(owners, row_experts, 1, model_width)).astype(
        jnp.bfloat16
    )
    mixed = combine(
        frames,
        returned.reshape(expert_total * capacity, model_width),
        slot_index,
        kept_mask,
        gate_codes,
    )
    return (mixed, load_total)


def solution(mesh):
    split = Mesh(mesh.devices.reshape(4, 2, 4, 4), ("dp_0", "dp_1", "expert_0", "expert_1"))
    in_specs = (
        P(DP_EXPERT, None),
        P(),
        P(),
        P(DP_EXPERT, None),
        P(DP_EXPERT, None),
        P(),
        P(DP_EXPERT, None, None),
        P(DP_EXPERT, None),
        P(DP_EXPERT, None, None),
        P(),
    )
    out_specs = (P(DP_EXPERT, None), P())
    return jax.shard_map(
        per_device, mesh=split, in_specs=in_specs, out_specs=out_specs, check_vma=False
    )
```

profile of v0, /device:TPU:0, one launch (start us, length us, event | category | flops | bytes accessed | tf_op | source)
XLA Modules:
  0.0 186.2 jit_solution(15559914447750488012)
XLA Ops:
  0.6 0.0 copy-start
  0.6 0.9 copy.30
  1.6 0.1 reshape.188
  1.7 0.1 eq.39
  1.9 0.6 reduce-window.6
  2.5 0.2 slice_reduce_fusion
  2.7 0.8 select_reduce_fusion.2
  3.5 0.2 select_reduce_fusion
  3.7 0.1 reduce_sum.104
  3.8 1.1 convert_reduce_fusion.1
  4.9 1.2 fusion.22
  6.1 0.1 convert_element_type.84
  6.2 1.2 fusion.25
  7.4 2.1 %gather_fusion = bf16[512,1024]{1,0:T(8,128)(2,1)S(1)} fusion(bf16[128,1024]{1,0:T(8,128)(2,1)S(1)} %fusion.25, s32[1024]{0:T(1024)S(1)} %pad_clamp_fusion.1), kind=kCustom, calls=%fused_computation | custom fusion | bytes 2099200 | tf_op jit(solution)/shard_map/jit(_take)/gather | solution.py:48
  9.5 0.2 select_multiply_fusion
  9.7 0.5 broadcast_in_dim.22
  10.3 0.0 copy-start.5
  10.3 62.1 %all_to_all.21 = bf16[128,16,1024]{2,1,0:T(8,128)(2,1)} all-to-all(bf16[128,16,1024]{2,1,0:T(8,128)(2,1)S(1)} %bitcast.41), channel_id=1, replica_groups=mesh['dp_0'=4,'dp_1'=2,'expert_0'=4,'expert_1'=4] {'dp_0','dp_1','expert..., dimensions={0} | all-to-all | bytes 8388608 | tf_op jit(solution)/shard_map/all_to_all | solution.py:90
  72.4 0.0 copy-done
  72.4 0.0 copy-done.5
  72.4 28.5 %fusion.12 = bf16[2048,1024]{1,0:T(8,128)(2,1)} fusion(f32[1024]{0:T(1024)S(1)} %bitcast.49, bf16[2048,1024]{1,0:T(8,128)(2,1)} %bitcast.44, bf16[1,1024,1024]{2,1,0:T(8,128)(2,1)S(1)} %copy-done, bf16[1,1024,1024]{2,1,0:T(8,128)(2,1)} %param.16), kind=kOutput, calls=%fused_computation.23 | convolution fusion | flops 8730443776 | bytes 12587008 | tf_op jit(solution)/shard_map/dot_general | solution.py:101
  100.9 0.0 copy-start.2
  100.9 0.0 copy-start.3
  100.9 0.0 copy-start.4
  100.9 6.5 %all-to-all-start.1 = ((bf16[128,16,1024]{2,1,0:T(8,128)(2,1)}), bf16[128,16,1024]{2,1,0:T(8,128)(2,1)}, u32[]{:S(2)}, u32[]{:S(2)}) async-start(bf16[128,16,1024]{2,1,0:T(8,128)(2,1)} %bitcast.43), calls=%async_computation.1 | async-start | bytes 8388608 | tf_op jit(solution)/shard_map/all_to_all | solution.py:104
  107.4 0.1 reduce_sum.101
  107.6 0.1 reduce_sum.112
  107.7 0.0 copy-done.2
  107.8 0.0 copy-done.3
  107.8 0.1 copy.35
  107.9 0.1 mul.144
  108.0 0.1 copy.33
  108.1 0.1 copy.37
  108.2 0.0 copy-done.4
  108.2 0.1 copy.38
  108.4 0.1 copy.34
  108.5 0.1 select_reduce_fusion.1
  108.6 36.8 %psum.28 = s32[32]{0:T(128)S(1)} all-reduce(s32[32]{0:T(128)S(1)} %select_reduce_fusion.1), channel_id=1, replica_groups=mesh['dp_0'=4,'dp_1'=2,'expert_0'=4,'expert_1'=4] {'dp_0'}, use_global_device_ids=true, to_apply=%region_12.13 | all-reduce | flops 32 | bytes 256 | tf_op jit(solution)/shard_map/psum | solution.py:17
  145.4 1.8 psum.29
  147.3 19.3 %psum.30 = s32[32]{0:T(128)S(1)} all-reduce(s32[32]{0:T(128)S(1)} %psum.29), channel_id=1, replica_groups=mesh['dp_0'=4,'dp_1'=2,'expert_0'=4,'expert_1'=4] {'expert_0'}, use_global_device_ids=true, to_apply=%region_14.15 | all-reduce | flops 32 | bytes 256 | tf_op jit(solution)/shard_map/psum | solution.py:17
  166.5 10.3 %psum.31 = s32[32]{0:T(128)} all-reduce(s32[32]{0:T(128)S(1)} %psum.30), channel_id=1, replica_groups=mesh['dp_0'=4,'dp_1'=2,'expert_0'=4,'expert_1'=4] {'expert_1'}, use_global_device_ids=true, to_apply=%region_15.16 | all-reduce | flops 32 | bytes 256 | tf_op jit(solution)/shard_map/psum | solution.py:17
  176.8 0.0 all-to-all-done.1
  176.8 3.4 %convert_reduce_fusion = f32[8,4,16,1024]{3,2,1,0:T(8,128)S(1)} fusion(bf16[128,16,1024]{2,1,0:T(8,128)(2,1)} %all-to-all-done.1), kind=kLoop, calls=%fused_computation.6 | loop fusion | flops 3670016 | bytes 6291456 | tf_op jit(solution)/shard_map/reduce_sum | solution.py:105
  180.3 0.3 add_convert_fusion
  180.6 0.0 copy-start.1
  180.6 2.0 %gather_fusion.1 = bf16[256,1024]{1,0:T(8,128)(2,1)} fusion(bf16[512,1024]{1,0:T(8,128)(2,1)S(1)} %bitcast.40, s32[1024]{0:T(1024)S(1)} %pad_clamp_fusion), kind=kCustom, calls=%fused_computation.1 | custom fusion | bytes 1049600 | tf_op jit(solution)/shard_map/jit(_take)/gather | solution.py:56
  182.6 1.2 gather.15
  183.8 1.6 multiply_reduce_fusion
  185.4 0.0 copy-done.1
  185.5 0.8 fusion.27
  (19 shorter events, 0.2 us)
Async XLA Ops:
  0.6 71.8 %copy-start = (bf16[1,1024,1024]{2,1,0:T(8,128)(2,1)S(1)}, bf16[1,1024,1024]{2,1,0:T(8,128)(2,1)}, u32[]{:S(2)}) copy-start(bf16[1,1024,1024]{2,1,0:T(8,128)(2,1)} %param.18) | copy-start | bytes 6291460
  10.3 62.2 %copy-start.5 = (f32[1,1024]{1,0:T(1,128)S(1)}, f32[1,1024]{1,0:T(1,128)}, u32[]{:S(2)}) copy-start(f32[1,1024]{1,0:T(1,128)} %param.17) | copy-start | bytes 12292
  100.9 6.8 %copy-start.2 = (f32[32,1024]{1,0:T(8,128)S(1)}, f32[32,1024]{1,0:T(8,128)}, u32[]{:S(2)}) copy-start(f32[32,1024]{1,0:T(8,128)} %param.19) | copy-start | bytes 393220
  100.9 6.8 %copy-start.3 = (s32[128,2]{0,1:T(2,128)S(1)}, s32[128,2]{0,1:T(2,128)}, u32[]{:S(2)}) copy-start(s32[128,2]{0,1:T(2,128)} %param.13) | copy-start | bytes 3076
  100.9 7.2 %copy-start.4 = (s32[128,2]{0,1:T(2,128)S(1)}, s32[128,2]{0,1:T(2,128)}, u32[]{:S(2)}) copy-start(s32[128,2]{0,1:T(2,128)} %param.14) | copy-start | bytes 3076
  100.9 75.9 %all-to-all-start.1 = ((bf16[128,16,1024]{2,1,0:T(8,128)(2,1)}), bf16[128,16,1024]{2,1,0:T(8,128)(2,1)}, u32[]{:S(2)}, u32[]{:S(2)}) async-start(bf16[128,16,1024]{2,1,0:T(8,128)(2,1)} %bitcast.43), calls=%async_computation.1 | async-start | bytes 8388608 | tf_op jit(solution)/shard_map/all_to_all | solution.py:104
  180.6 4.8 %copy-start.1 = (bf16[128,1024]{1,0:T(8,128)(2,1)S(1)}, bf16[128,1024]{1,0:T(8,128)(2,1)}, u32[]{:S(2)}) copy-start(bf16[128,1024]{1,0:T(8,128)(2,1)} %param.10) | copy-start | bytes 786436
where the time goes:
time: 187 us; the launch traced here: 186 us
  blocking collectives  130 us (70%)
  matrix products  28.5 us (15%)
  other arithmetic  11.7 us (6%)
  local copies, waits for them, and re-layouts  8.34 us (4%)
  starting transfers between devices  6.48 us (3%)
    psum x4, blocking collectives, over_axes(): value = lax.psum(value, axis)  68.2 us
    all_to_all x1, blocking collectives, per_device(): lax.all_to_all(copies.reshape(owners * holders * capacity, model_width),...  62.1 us
    dot_general x1, matrix products, per_device(): jnp.dot(hidden, down_weight[0], preferred_element_type=jnp.float32)  28.5 us
    all_to_all x1, starting transfers between devices, per_device(): lax.all_to_all(partial_out, DP_EXPERT, split_axis=0, concat_axis=0, tiled...  6.48 us
  transfers between devices with their start and end apart: 1, of which 0 were waited for; matrix products, arithmetic and copies ran while one was open for 1% of the time, Pallas kernels for 0%

commit v1 on v0

v1 whole, which is shorter than its diff:
```python
import random

import jax
import jax.numpy as jnp
from jax import lax
from jax.experimental import pallas as pl
from jax.experimental.pallas import tpu as pltpu
from jax.sharding import PartitionSpec as P

MESH = pl.DeviceIdType.MESH
EPS = 1e-05
D = 1024
FRAMES = 128
CAP = 16
PEERS = 32
CB = 256
CA = D - CB
CHUNKS = 4
PER = PEERS // CHUNKS
HALF = PER // 2
ROWS = 4 * PER * CAP
TILE = 256


def plane_order():
    rest = list(range(1, PEERS))
    random.Random(2).shuffle(rest)
    return [0] + rest


ORDER = plane_order()
OFFSETS = [((n // 2) % 4, n // 8, n % 2) for n in range(PEERS)]


def kernel(
    frames,
    gain,
    nbias,
    routes,
    codes,
    limits,
    up_hbm,
    up_b,
    down_hbm,
    down_b,
    mixed,
    load,
    up,
    down,
    slots_a,
    norm_b,
    slots_b,
    x_in,
    hid,
    part,
    t_r,
    t_l,
    g_l,
    g_r,
    e_out,
    ret_a,
    ret_b,
    y_out,
    y_in,
    info,
    cnt_out,
    cnt_in,
    brow,
    w_sem,
    send,
    r_a,
    r_b,
    r_info,
    r_nb,
    f_l,
    f_r,
    h_l,
    h_r,
    rt_r,
    rt_l,
    rg_l,
    rg_r,
    r_ra,
    r_rb,
    r_y,
    r_cnt,
):
    dp = lax.axis_index("dp")
    ex = lax.axis_index("expert")
    x, y = lax.rem(ex, 4), lax.div(ex, 4)
    z, c = lax.div(dp, 2), lax.rem(dp, 2)
    mine = dp * 4 + y

    def plane(n):
        dy, dz, dc = OFFSETS[n]
        return (
            lax.rem(z + dz, 4) * 2 + lax.rem(c + dc, 2),
            lax.rem(y + dy, 4) * 4 + x,
        )

    def source(n):
        dy, dz, dc = OFFSETS[n]
        return (
            lax.rem(z + 4 - dz, 4) * 2 + lax.rem(c + 2 - dc, 2),
            lax.rem(y + 4 - dy, 4) * 4 + x,
        )

    def along(k):
        return (dp, y * 4 + lax.rem(x + k, 4))

    def put(src, dst, s, r, where):
        pltpu.make_async_remote_copy(
            src, dst, s, r, device_id=where, device_id_type=MESH
        ).start()

    def arrived(ref, sem):
        pltpu.make_async_copy(ref, ref, sem).wait()

    barrier = pltpu.get_barrier_semaphore()
    for n in range(1, PEERS):
        pl.semaphore_signal(barrier, inc=1, device_id=plane(n), device_id_type=MESH)
    for k in range(1, 4):
        pl.semaphore_signal(barrier, inc=1, device_id=along(k), device_id_type=MESH)
    up_copy = pltpu.make_async_copy(up_hbm.at[0], up, w_sem.at[0])
    down_copy = pltpu.make_async_copy(down_hbm.at[0], down, w_sem.at[1])
    up_copy.start()
    down_copy.start()

    values = frames[...].astype(jnp.float32)
    center = jnp.mean(values, axis=-1, keepdims=True)
    shifted = values - center
    spread = jnp.mean(shifted * shifted, axis=-1, keepdims=True)
    normed = (shifted * lax.rsqrt(spread + EPS) * gain[...] + nbias[...]).astype(jnp.bfloat16)
    norm_b[0] = normed[:, CA:]

    chosen = routes[...]
    ids = lax.broadcasted_iota(jnp.int32, (FRAMES, FRAMES), 0)
    cols = lax.broadcasted_iota(jnp.int32, (FRAMES, FRAMES), 1)
    hit0 = (ids == chosen[0:1, :]).astype(jnp.float32)
    hit1 = (ids == chosen[1:2, :]).astype(jnp.float32)
    before = (ids < cols).astype(jnp.bfloat16)
    earlier = jnp.dot(
        (hit0 + hit1).astype(jnp.bfloat16), before, preferred_element_type=jnp.float32
    )
    rank = jnp.concatenate(
        [
            jnp.sum(earlier * hit0, axis=0, keepdims=True),
            jnp.sum(earlier * hit1, axis=0, keepdims=True),
        ],
        axis=0,
    ).astype(jnp.int32)
    bound = jnp.zeros((2, FRAMES), jnp.int32)
    for e in range(32):
        bound = jnp.where(chosen == e, limits[e], bound)
    kept = rank < bound
    dz = (lax.shift_right_logical(chosen, 3) - z + 4) & 3
    dc = ((lax.shift_right_logical(chosen, 2) & 1) - c + 2) & 1
    dy = ((chosen & 3) - y + 4) & 3
    spot = jnp.where(kept, ((dz * 4 + dy) * 2 + dc) * CAP + rank, -1)
    keptf = kept.astype(jnp.float32)
    taken = (hit0 * keptf[0:1, :] + hit1 * keptf[1:2, :]).astype(jnp.bfloat16)
    counts = lax.dot_general(
        jnp.ones((8, FRAMES), jnp.bfloat16),
        taken,
        (((1,), (1,)), ((), ())),
        preferred_element_type=jnp.float32,
    ).astype(jnp.int32)
    info[0, 0:2, :] = spot
    info[0, 2:4, :] = codes[...]
    info[0, 4:8, :] = counts[0:4, :]

    slot_ids = lax.broadcasted_iota(jnp.int32, (PEERS * CAP, FRAMES), 0)

    def gathered(k, rows):
        spots = info[k]
        pick = (slot_ids == spots[0:1, :]) | (slot_ids == spots[1:2, :])
        return (
            jnp.dot(
                pick.astype(jnp.float32).astype(jnp.bfloat16),
                rows,
                preferred_element_type=jnp.float32,
            )
            .astype(jnp.bfloat16)
            .reshape(PEERS, CAP, rows.shape[1])
        )

    slots_a[...] = gathered(0, normed[:, :CA])
    row = down_b[pl.ds(mine, 1), :]
    lane = lax.broadcasted_iota(jnp.int32, (1, D), 1)
    brow[...] = jnp.where(lane >= CA, row * 0.25, 0.0)

    pl.semaphore_wait(barrier, PEERS - 1 + 3)
    for k in range(1, 4):
        put(info.at[0], info.at[k], send.at[0], r_info.at[k - 1], along(k))
        put(norm_b.at[0], norm_b.at[k], send.at[1], r_nb.at[k - 1], along(k))
    for p in range(1, PEERS):
        n = ORDER[p]
        put(
            slots_a.at[n],
            x_in.at[0, p, :, pl.ds(0, CA)],
            send.at[2],
            r_a.at[p // PER],
            plane(n),
        )
    x_in[0, 0, :, :CA] = slots_a[0]

    slots_b[0] = gathered(0, normed[:, CA:])
    total = info[0, 4:5, :]
    for k in range(1, 4):
        arrived(info.at[k], r_info.at[k - 1])
        arrived(norm_b.at[k], r_nb.at[k - 1])
        slots_b[k] = gathered(k, norm_b[k])
        total = total + info[k, 4:5, :]
    cnt_out[...] = total
    for p in range(1, PEERS):
        n = ORDER[p]
        put(
            slots_b.at[:, n],
            x_in.at[:, p, :, pl.ds(CA, CB)],
            send.at[3],
            r_b.at[p // PER],
            plane(n),
        )
        put(cnt_out, cnt_in.at[n], send.at[4], r_cnt, plane(n))
    x_in[:, 0, :, CA:] = slots_b[:, 0]

    def chunk(j):
        return pl.ds(j * PER, PER)

    def first(j):
        return pl.ds(j * PER, HALF)

    def second(j):
        return pl.ds(j * PER + HALF, HALF)

    wide = pl.ds(0, CA)
    narrow = pl.ds(CA, CB)

    def own(j):
        begin = max(j * PER, 1)
        spots = pl.ds(begin, (j + 1) * PER - begin)
        arrived(x_in.at[0, spots, :, wide], r_a.at[j])
        put(
            x_in.at[0, chunk(j), :, wide],
            x_in.at[1, chunk(j), :, wide],
            send.at[5],
            f_l.at[j],
            along(1),
        )
        put(
            x_in.at[0, chunk(j), :, wide],
            x_in.at[3, chunk(j), :, wide],
            send.at[6],
            f_r.at[j],
            along(3),
        )

    def forward(j):
        arrived(x_in.at[1, chunk(j), :, wide], f_l.at[j])
        put(
            x_in.at[1, first(j), :, wide],
            x_in.at[2, first(j), :, wide],
            send.at[7],
            h_l.at[j],
            along(1),
        )
        arrived(x_in.at[3, chunk(j), :, wide], f_r.at[j])
        put(
            x_in.at[3, second(j), :, wide],
            x_in.at[2, second(j), :, wide],
            send.at[8],
            h_r.at[j],
            along(3),
        )

    def ready(j):
        begin = max(j * PER, 1)
        spots = pl.ds(begin, (j + 1) * PER - begin)
        arrived(x_in.at[:, spots, :, narrow], r_b.at[j])
        arrived(x_in.at[2, first(j), :, wide], h_l.at[j])
        arrived(x_in.at[2, second(j), :, wide], h_r.at[j])

    def project_up(j):
        def step(t, carry):
            lanes = pl.ds(pl.multiple_of(t * TILE, TILE), TILE)
            rows = x_in[:, j * PER : (j + 1) * PER].reshape(ROWS, D)
            pre = jnp.dot(rows, up[:, lanes], preferred_element_type=jnp.float32)
            pre = pre + up_b[:, lanes]
            act = 0.5 * pre * (1.0 + lax.erf(pre * 0.7071067811865476))
            hid[:, lanes] = act.astype(jnp.bfloat16)
            return carry

        lax.fori_loop(0, D // TILE, step, 0)

    def project_down(j):
        def step(t, carry):
            lanes = pl.ds(pl.multiple_of(t * TILE, TILE), TILE)
            out = jnp.dot(hid[...], down[:, lanes], preferred_element_type=jnp.float32)
            out = out + brow[:, lanes]
            part[:, j * PER : (j + 1) * PER, :, lanes] = out.astype(jnp.bfloat16).reshape(
                4, PER, CAP, TILE
            )
            return carry

        lax.fori_loop(0, D // TILE, step, 0)

    def give_back(j):
        put(part.at[2, first(j), :, wide], t_r.at[j], send.at[9], rt_r.at[j], along(1))
        put(part.at[2, second(j), :, wide], t_l.at[j], send.at[10], rt_l.at[j], along(3))
        put(part.at[3, second(j), :, wide], g_l.at[second(j)], send.at[11], rg_l.at[j], along(1))
        put(part.at[1, first(j), :, wide], g_r.at[first(j)], send.at[12], rg_r.at[j], along(3))
        for p in range(j * PER, (j + 1) * PER):
            if p:
                put(
                    part.at[:, p, :, narrow],
                    ret_b.at[:, ORDER[p]],
                    send.at[13],
                    r_rb,
                    source(ORDER[p]),
                )
            else:
                ret_b[:, 0] = part[:, 0, :, CA:]

    def add_on(j):
        arrived(t_r.at[j], rt_r.at[j])
        spots = slice(j * PER, j * PER + HALF)
        part[3, spots, :, :CA] = (
            part[3, spots, :, :CA].astype(jnp.float32) + t_r[j].astype(jnp.float32)
        ).astype(jnp.bfloat16)
        put(part.at[3, first(j), :, wide], g_l.at[first(j)], send.at[11], rg_l.at[j], along(1))
        arrived(t_l.at[j], rt_l.at[j])
        spots = slice(j * PER + HALF, (j + 1) * PER)
        part[1, spots, :, :CA] = (
            part[1, spots, :, :CA].astype(jnp.float32) + t_l[j].astype(jnp.float32)
        ).astype(jnp.bfloat16)
        put(part.at[1, second(j), :, wide], g_r.at[second(j)], send.at[12], rg_r.at[j], along(3))

    def finish(j):
        arrived(g_l.at[chunk(j)], rg_l.at[j])
        arrived(g_r.at[chunk(j)], rg_r.at[j])
        spots = slice(j * PER, (j + 1) * PER)
        bias = row[:, :CA].reshape(1, 1, CA)
        e_out[spots] = (
            part[0, spots, :, :CA].astype(jnp.float32)
            + g_l[spots].astype(jnp.float32)
            + g_r[spots].astype(jnp.float32)
            + bias
        ).astype(jnp.bfloat16)
        for p in range(j * PER, (j + 1) * PER):
            if p:
                put(e_out.at[p], ret_a.at[ORDER[p]], send.at[14], r_ra, source(ORDER[p]))
            else:
                ret_a[0] = e_out[0]

    own(0)
    own(1)
    forward(0)
    own(2)
    forward(1)
    own(3)
    up_copy.wait()
    down_copy.wait()
    ready(0)
    project_up(0)
    forward(2)
    project_down(0)
    give_back(0)
    forward(3)
    ready(1)
    project_up(1)
    add_on(0)
    project_down(1)
    give_back(1)
    finish(0)
    ready(2)
    project_up(2)
    add_on(1)
    project_down(2)
    give_back(2)
    finish(1)
    ready(3)
    project_up(3)
    add_on(2)
    project_down(3)
    give_back(3)
    finish(2)
    add_on(3)
    finish(3)

    arrived(cnt_in.at[pl.ds(1, PEERS - 1)], r_cnt)
    cnt_in[0] = cnt_out[...]
    load[...] = jnp.sum(cnt_in[...], axis=0)[:, :32]

    slot_cols = lax.broadcasted_iota(jnp.int32, (FRAMES, PEERS * CAP), 1)

    def combined(k, rows):
        table = jnp.concatenate([info[k], jnp.zeros((FRAMES - 8, FRAMES), jnp.int32)], axis=0)
        turned = jnp.transpose(table.astype(jnp.float32))
        code0, code1 = turned[:, 2:3], turned[:, 3:4]
        weight0 = code0 / (code0 + code1)
        weight1 = code1 / (code0 + code1)
        spots = turned.astype(jnp.int32)
        pick0 = (slot_cols == spots[:, 0:1]).astype(jnp.float32).astype(jnp.bfloat16)
        pick1 = (slot_cols == spots[:, 1:2]).astype(jnp.float32).astype(jnp.bfloat16)
        out0 = jnp.dot(pick0, rows, preferred_element_type=jnp.float32)
        out1 = jnp.dot(pick1, rows, preferred_element_type=jnp.float32)
        return out0 * weight0 + out1 * weight1

    arrived(ret_b.at[:, pl.ds(1, PEERS - 1)], r_rb)
    for k in range(1, 4):
        y_out[k - 1] = combined(k, ret_b[k].reshape(PEERS * CAP, CB)).astype(jnp.bfloat16)
        put(y_out.at[k - 1], y_in.at[k - 1], send.at[15], r_y.at[k - 1], along(4 - k))
    own_b = combined(0, ret_b[0].reshape(PEERS * CAP, CB))
    arrived(ret_a.at[pl.ds(1, PEERS - 1)], r_ra)
    own_a = combined(0, ret_a[...].reshape(PEERS * CAP, CA))
    mixed[:, :CA] = (frames[:, :CA].astype(jnp.float32) + own_a).astype(jnp.bfloat16)
    for k in range(1, 4):
        arrived(y_in.at[k - 1], r_y.at[k - 1])
        own_b = own_b + y_in[k - 1].astype(jnp.float32)
    mixed[:, CA:] = (frames[:, CA:].astype(jnp.float32) + own_b).astype(jnp.bfloat16)

    rest = pl.ds(1, PEERS - 1)
    some = pl.ds(1, 3)
    halves = pl.ds(0, PEERS // 2)
    arrived(info.at[some], send.at[0])
    arrived(norm_b.at[some], send.at[1])
    arrived(slots_a.at[rest], send.at[2])
    arrived(slots_b.at[:, rest], send.at[3])
    arrived(cnt_in.at[rest], send.at[4])
    arrived(e_out, send.at[5])
    arrived(e_out, send.at[6])
    arrived(e_out.at[halves], send.at[7])
    arrived(e_out.at[halves], send.at[8])
    arrived(e_out.at[halves], send.at[9])
    arrived(e_out.at[halves], send.at[10])
    arrived(e_out, send.at[11])
    arrived(e_out, send.at[12])
    arrived(slots_b.at[:, rest], send.at[13])
    arrived(slots_a.at[rest], send.at[14])
    arrived(y_out, send.at[15])


def per_device(frames, gain, nbias, routes, codes, limits, up_w, up_b, down_w, down_b):
    vmem = pl.BlockSpec(memory_space=pltpu.VMEM)
    hbm = pl.BlockSpec(memory_space=pl.ANY)
    smem = pl.BlockSpec(memory_space=pltpu.SMEM)
    bf16, f32, i32 = jnp.bfloat16, jnp.float32, jnp.int32
    dma = pltpu.SemaphoreType.DMA
    mixed, load = pl.pallas_call(
        kernel,
        out_shape=(
            jax.ShapeDtypeStruct((FRAMES, D), bf16),
            jax.ShapeDtypeStruct((1, 32), i32),
        ),
        in_specs=[vmem, vmem, vmem, vmem, vmem, smem, hbm, vmem, hbm, vmem],
        out_specs=(vmem, vmem),
        scratch_shapes=[
            pltpu.VMEM((D, D), bf16),
            pltpu.VMEM((D, D), bf16),
            pltpu.VMEM((PEERS, CAP, CA), bf16),
            pltpu.VMEM((4, FRAMES, CB), bf16),
            pltpu.VMEM((4, PEERS, CAP, CB), bf16),
            pltpu.VMEM((4, PEERS, CAP, D), bf16),
            pltpu.VMEM((ROWS, D), bf16),
            pltpu.VMEM((4, PEERS, CAP, D), bf16),
            pltpu.VMEM((CHUNKS, HALF, CAP, CA), bf16),
            pltpu.VMEM((CHUNKS, HALF, CAP, CA), bf16),
            pltpu.VMEM((PEERS, CAP, CA), bf16),
            pltpu.VMEM((PEERS, CAP, CA), bf16),
            pltpu.VMEM((PEERS, CAP, CA), bf16),
            pltpu.VMEM((PEERS, CAP, CA), bf16),
            pltpu.VMEM((4, PEERS, CAP, CB), bf16),
            pltpu.VMEM((3, FRAMES, CB), bf16),
            pltpu.VMEM((3, FRAMES, CB), bf16),
            pltpu.VMEM((4, 8, FRAMES), i32),
            pltpu.VMEM((1, FRAMES), i32),
            pltpu.VMEM((PEERS, 1, FRAMES), i32),
            pltpu.VMEM((1, D), f32),
            dma((2,)),
            dma((16,)),
            dma((CHUNKS,)),
            dma((CHUNKS,)),
            dma((3,)),
            dma((3,)),
            dma((CHUNKS,)),
            dma((CHUNKS,)),
            dma((CHUNKS,)),
            dma((CHUNKS,)),
            dma((CHUNKS,)),
            dma((CHUNKS,)),
            dma((CHUNKS,)),
            dma((CHUNKS,)),
            dma,
            dma,
            dma((3,)),
            dma,
        ],
        compiler_params=pltpu.CompilerParams(
            collective_id=0, has_side_effects=True, vmem_limit_bytes=56 << 20
        ),
        name="moe",
    )(
        frames,
        gain.reshape(1, D),
        nbias.reshape(1, D),
        routes.T,
        codes.T,
        limits,
        up_w,
        up_b,
        down_w,
        down_b,
    )
    return mixed, load.reshape(32)


def solution(mesh):
    both = ("dp", "expert")
    in_specs = (
        P(both, None),
        P(),
        P(),
        P(both, None),
        P(both, None),
        P(),
        P(both, None, None),
        P(both, None),
        P(both, None, None),
        P(),
    )
    out_specs = (P(both, None), P())
    return jax.shard_map(
        per_device, mesh=mesh, in_specs=in_specs, out_specs=out_specs, check_vma=False
    )
```

time: 187 us -> 83.9 us (0.45)
  blocking collectives: 130 us -> 0 us
  Pallas kernels: 0 us -> 80.3 us
  matrix products: 28.5 us -> 0 us
  other arithmetic: 11.7 us -> 0 us
  starting transfers between devices: 6.48 us -> 0 us
  local copies, waits for them, and re-layouts: 8.34 us -> 2.8 us
    pallas_call x0 -> x1, Pallas kernels: none -> 80.3 us  [per_device(): pl.pallas_call(kernel, out_shape=(jax.ShapeDtypeStruct((FRAMES, D), bf16)...]
    psum x4 -> x0, blocking collectives: 68.2 us -> none  [over_axes(): value = lax.psum(value, axis)]
    all_to_all x1 -> x0, blocking collectives: 62.1 us -> none  [per_device(): lax.all_to_all(copies.reshape(owners * holders * capacity, model_width),...]
    dot_general x1 -> x0, matrix products: 28.5 us -> none  [per_device(): jnp.dot(hidden, down_weight[0], preferred_element_type=jnp.float32)]
    reduce_sum x8 -> x0, other arithmetic: 8.44 us -> none  [the longest x1 3.44 us: per_device(): jnp.sum(back.reshape(owners, row_experts, groups, capacity, model_width)....]
    all_to_all x1 -> x0, starting transfers between devices: 6.48 us -> none  [per_device(): lax.all_to_all(partial_out, DP_EXPERT, split_axis=0, concat_axis=0, tiled...]
    gather x3 -> x0, local copies, waits for them, and re-layouts: 5.25 us -> none  [the longest x2 3.19 us: combine(): picked = jnp.take(returned, slot_index, axis=0).astype(jnp.float32)]
    convert_element_type x6 -> x0, other arithmetic: 2.32 us -> none  [the longest x1 1.21 us: layer_norm(): (shifted * lax.rsqrt(spread + epsilon) * norm_gain + norm_bias).astype(jn...]
  transfers between devices with their start and end apart: 1 -> 0, of which waited for: 0 -> 0; matrix products, arithmetic and copies ran while one was open for 1% -> 0% of each run, Pallas kernels for 0% -> 0%
where the time goes in v1:
time: 83.9 us; the launch traced here: 83.7 us
  Pallas kernels  80.3 us (96%)
  local copies, waits for them, and re-layouts  2.8 us (3%)
    pallas_call x1, Pallas kernels, per_device(): pl.pallas_call(kernel, out_shape=(jax.ShapeDtypeStruct((FRAMES, D), bf16)...  80.3 us
    unnamed x2, local copies, waits for them, and re-layouts  2.8 us

profile of v1, /device:TPU:0, one launch (start us, length us, event | category | flops | bytes accessed | tf_op | source)
XLA Modules:
  0.0 83.7 jit_solution(17197182776473621318)
XLA Ops:
  0.6 80.3 %moe.1 = (bf16[128,1024]{1,0:T(8,128)(2,1)}, s32[1,32]{1,0:T(1,128)}) custom-call(bf16[128,1024]{1,0:T(8,128)(2,1)} %frames.1, f32[1,1024]{1,0:T(1,128)} %bitcast.5, f32[1,1024]{1,0:T(1,128)} %bitcast.6, s32[2,128]{1,0:T(2,128)} %bitcast.7, s32[2,128]{1,0:T(2,128)} %bitcast.8, s32[32]{0:T(128)} %limits.1, bf16[1,1024,1024]{2,1,0:T(8,128)(2,1)} %up_hbm.1, ...), custom_call_target="tpu_custom_call" | custom-call | tf_op jit(solution)/shard_map/moe/pallas_call | solution.py:449
  80.9 1.7 %copy.14 = bf16[128,1024]{1,0:T(8,128)(2,1)} copy(bf16[128,1024]{1,0:T(8,128)(2,1)} %get-tuple-element.8) | data formatting | bytes 524288
  82.6 1.1 %copy.15 = s32[32]{0:T(128)} copy(s32[32]{0:T(128)} %bitcast.9) | data formatting | bytes 256

commit v2 on v1

v2 whole, which is shorter than its diff:
```python
import random

import jax
import jax.numpy as jnp
from jax import lax
from jax.experimental import pallas as pl
from jax.experimental.pallas import tpu as pltpu
from jax.sharding import PartitionSpec as P

MESH = pl.DeviceIdType.MESH
EPS = 1e-05
D = 1024
FRAMES = 128
CAP = 16
PEERS = 32
CB = 384
CA = D - CB
SIZES = [8, 8, 8, 8]
CHUNKS = len(SIZES)
STARTS = [sum(SIZES[:j]) for j in range(CHUNKS + 1)]
CHUNK_OF = [j for j in range(CHUNKS) for _ in range(SIZES[j])]
TILE = 256


def plane_order():
    rest = list(range(1, PEERS))
    random.Random(5).shuffle(rest)
    return [0] + rest


ORDER = plane_order()
SCHEDULE = (
    "own0 gath0 send0 own1 fwd0 own2 fwd1 own3 wts0 "
    "ready0 up0 fwd2 down0 give0 ready1 up1 fwd3 down1 give1 add0 "
    "ready2 up2 down2 give2 add1 ready3 up3 down3 give3 fin0 add2 fin1 add3 fin2 fin3"
)
OFFSETS = [((n // 2) % 4, n // 8, n % 2) for n in range(PEERS)]


def kernel(
    frames_hbm,
    gain_hbm,
    nbias_hbm,
    routes_hbm,
    codes_hbm,
    limits_hbm,
    up_hbm,
    up_b_hbm,
    down_hbm,
    down_b_hbm,
    mixed,
    load,
    frames,
    gain,
    nbias,
    routes,
    codes,
    limits,
    up_b,
    down_b,
    up,
    down,
    slots_a,
    norm_b,
    slots_b,
    x_in,
    hid,
    part,
    t_r,
    t_l,
    g_l,
    g_r,
    e_out,
    ret_a,
    ret_b,
    y_out,
    y_in,
    info,
    cnt_out,
    cnt_in,
    brow,
    w_sem,
    send,
    r_a,
    r_b,
    r_info,
    r_nb,
    f_l,
    f_r,
    h_l,
    h_r,
    rt_r,
    rt_l,
    rg_l,
    rg_r,
    r_ra,
    r_rb,
    r_y,
    r_cnt,
):
    dp = lax.axis_index("dp")
    ex = lax.axis_index("expert")
    x, y = lax.rem(ex, 4), lax.div(ex, 4)
    z, c = lax.div(dp, 2), lax.rem(dp, 2)
    mine = dp * 4 + y

    def plane(n):
        dy, dz, dc = OFFSETS[n]
        return (
            lax.rem(z + dz, 4) * 2 + lax.rem(c + dc, 2),
            lax.rem(y + dy, 4) * 4 + x,
        )

    def source(n):
        dy, dz, dc = OFFSETS[n]
        return (
            lax.rem(z + 4 - dz, 4) * 2 + lax.rem(c + 2 - dc, 2),
            lax.rem(y + 4 - dy, 4) * 4 + x,
        )

    def along(k):
        return (dp, y * 4 + lax.rem(x + k, 4))

    def put(src, dst, s, r, where):
        pltpu.make_async_remote_copy(
            src, dst, s, r, device_id=where, device_id_type=MESH
        ).start()

    def arrived(ref, sem):
        pltpu.make_async_copy(ref, ref, sem).wait()

    with jax.named_scope("greet"):
        barrier = pltpu.get_barrier_semaphore()
        for n in range(1, PEERS):
            pl.semaphore_signal(barrier, inc=1, device_id=plane(n), device_id_type=MESH)
        for k in range(1, 4):
            pl.semaphore_signal(barrier, inc=1, device_id=along(k), device_id_type=MESH)
        loads = [
            pltpu.make_async_copy(src, dst, w_sem.at[i])
            for i, (src, dst) in enumerate(
                [
                    (frames_hbm, frames),
                    (gain_hbm, gain),
                    (nbias_hbm, nbias),
                    (routes_hbm, routes),
                    (codes_hbm, codes),
                    (limits_hbm, limits),
                    (down_b_hbm.at[pl.ds(pl.multiple_of(lax.div(mine, 8) * 8, 8), 8)], down_b),
                    (up_b_hbm, up_b),
                    (up_hbm.at[0], up),
                    (down_hbm.at[0], down),
                ]
            )
        ]
        for copy in loads:
            copy.start()
        for copy in loads[:6]:
            copy.wait()

    with jax.named_scope("norm"):
        values = frames[...].astype(jnp.float32)
        center = jnp.mean(values, axis=-1, keepdims=True)
        shifted = values - center
        spread = jnp.mean(shifted * shifted, axis=-1, keepdims=True)
        normed = (shifted * lax.rsqrt(spread + EPS) * gain[...] + nbias[...]).astype(jnp.bfloat16)
        norm_b[0] = normed[:, CA:]

    with jax.named_scope("route"):
        chosen = routes[...]
        ids = lax.broadcasted_iota(jnp.int32, (FRAMES, FRAMES), 0)
        cols = lax.broadcasted_iota(jnp.int32, (FRAMES, FRAMES), 1)
        hit0 = (ids == chosen[0:1, :]).astype(jnp.float32)
        hit1 = (ids == chosen[1:2, :]).astype(jnp.float32)
        before = (ids < cols).astype(jnp.bfloat16)
        earlier = jnp.dot(
            (hit0 + hit1).astype(jnp.bfloat16), before, preferred_element_type=jnp.float32
        )
        rank = jnp.concatenate(
            [
                jnp.sum(earlier * hit0, axis=0, keepdims=True),
                jnp.sum(earlier * hit1, axis=0, keepdims=True),
            ],
            axis=0,
        ).astype(jnp.int32)
        bound = jnp.zeros((2, FRAMES), jnp.int32)
        for e in range(32):
            bound = jnp.where(chosen == e, limits[e], bound)
        kept = rank < bound
        dz = (lax.shift_right_logical(chosen, 3) - z + 4) & 3
        dc = ((lax.shift_right_logical(chosen, 2) & 1) - c + 2) & 1
        dy = ((chosen & 3) - y + 4) & 3
        spot = jnp.where(kept, ((dz * 4 + dy) * 2 + dc) * CAP + rank, -1)
        keptf = kept.astype(jnp.float32)
        taken = (hit0 * keptf[0:1, :] + hit1 * keptf[1:2, :]).astype(jnp.bfloat16)
        counts = lax.dot_general(
            jnp.ones((8, FRAMES), jnp.bfloat16),
            taken,
            (((1,), (1,)), ((), ())),
            preferred_element_type=jnp.float32,
        ).astype(jnp.int32)
        info[0, 0:2, :] = spot
        info[0, 2:4, :] = codes[...]
        info[0, 4:8, :] = counts[0:4, :]

    slot_ids = lax.broadcasted_iota(jnp.int32, (PEERS * CAP, FRAMES), 0)

    def gathered(k, rows):
        spots = info[k]
        pick = (slot_ids == spots[0:1, :]) | (slot_ids == spots[1:2, :])
        return (
            jnp.dot(
                pick.astype(jnp.float32).astype(jnp.bfloat16),
                rows,
                preferred_element_type=jnp.float32,
            )
            .astype(jnp.bfloat16)
            .reshape(PEERS, CAP, rows.shape[1])
        )

    with jax.named_scope("gather"):
        slots_a[...] = gathered(0, normed[:, :CA])
        loads[6].wait()
        row = down_b[pl.ds(lax.rem(mine, 8), 1), :]
        lane = lax.broadcasted_iota(jnp.int32, (1, D), 1)
        brow[...] = jnp.where(lane >= CA, row * 0.25, 0.0)

    with jax.named_scope("met"):
        pl.semaphore_wait(barrier, PEERS - 1 + 3)
    with jax.named_scope("send_a"):
        for k in range(1, 4):
            put(info.at[0], info.at[k], send.at[0], r_info.at[k - 1], along(k))
            put(norm_b.at[0], norm_b.at[k], send.at[1], r_nb.at[k - 1], along(k))
        for p in range(1, PEERS):
            n = ORDER[p]
            put(
                slots_a.at[n],
                x_in.at[0, p, :, pl.ds(0, CA)],
                send.at[2],
                r_a.at[CHUNK_OF[p]],
                plane(n),
            )
        x_in[0, 0, :, :CA] = slots_a[0]

    def chunk(j):
        return pl.ds(STARTS[j], SIZES[j])

    def first(j):
        return pl.ds(STARTS[j], SIZES[j] // 2)

    def second(j):
        return pl.ds(STARTS[j] + SIZES[j] // 2, SIZES[j] // 2)

    def halves(j):
        return pl.ds(STARTS[j] // 2, SIZES[j] // 2)

    def remote(j):
        begin = max(STARTS[j], 1)
        return pl.ds(begin, STARTS[j + 1] - begin)

    wide = pl.ds(0, CA)
    narrow = pl.ds(CA, CB)

    def own(j):
        arrived(x_in.at[0, remote(j), :, wide], r_a.at[j])
        put(
            x_in.at[0, chunk(j), :, wide],
            x_in.at[1, chunk(j), :, wide],
            send.at[5],
            f_l.at[j],
            along(1),
        )
        put(
            x_in.at[0, chunk(j), :, wide],
            x_in.at[3, chunk(j), :, wide],
            send.at[6],
            f_r.at[j],
            along(3),
        )

    def forward(j):
        arrived(x_in.at[1, chunk(j), :, wide], f_l.at[j])
        put(
            x_in.at[1, first(j), :, wide],
            x_in.at[2, first(j), :, wide],
            send.at[7],
            h_l.at[j],
            along(1),
        )
        arrived(x_in.at[3, chunk(j), :, wide], f_r.at[j])
        put(
            x_in.at[3, second(j), :, wide],
            x_in.at[2, second(j), :, wide],
            send.at[8],
            h_r.at[j],
            along(3),
        )

    def ready(j):
        arrived(x_in.at[:, remote(j), :, narrow], r_b.at[j])
        arrived(x_in.at[2, first(j), :, wide], h_l.at[j])
        arrived(x_in.at[2, second(j), :, wide], h_r.at[j])

    def project_up(j):
        def step(t, carry):
            lanes = pl.ds(pl.multiple_of(t * TILE, TILE), TILE)
            rows = x_in[:, STARTS[j] : STARTS[j + 1]].reshape(4 * SIZES[j] * CAP, D)
            pre = jnp.dot(rows, up[:, lanes], preferred_element_type=jnp.float32)
            pre = pre + up_b[:, lanes]
            act = 0.5 * pre * (1.0 + lax.erf(pre * 0.7071067811865476))
            hid[: 4 * SIZES[j] * CAP, lanes] = act.astype(jnp.bfloat16)
            return carry

        lax.fori_loop(0, D // TILE, step, 0)

    def project_down(j):
        def step(t, carry):
            lanes = pl.ds(pl.multiple_of(t * TILE, TILE), TILE)
            out = jnp.dot(hid[: 4 * SIZES[j] * CAP], down[:, lanes], preferred_element_type=jnp.float32)
            out = out + brow[:, lanes]
            part[:, STARTS[j] : STARTS[j + 1], :, lanes] = out.astype(jnp.bfloat16).reshape(
                4, SIZES[j], CAP, TILE
            )
            return carry

        lax.fori_loop(0, D // TILE, step, 0)

    def give_back(j):
        put(part.at[2, first(j), :, wide], t_r.at[halves(j)], send.at[9], rt_r.at[j], along(1))
        put(part.at[2, second(j), :, wide], t_l.at[halves(j)], send.at[10], rt_l.at[j], along(3))
        put(part.at[3, second(j), :, wide], g_l.at[second(j)], send.at[11], rg_l.at[j], along(1))
        put(part.at[1, first(j), :, wide], g_r.at[first(j)], send.at[12], rg_r.at[j], along(3))
        for p in range(STARTS[j], STARTS[j + 1]):
            if p:
                put(
                    part.at[:, p, :, narrow],
                    ret_b.at[:, ORDER[p]],
                    send.at[13],
                    r_rb,
                    source(ORDER[p]),
                )
            else:
                ret_b[:, 0] = part[:, 0, :, CA:]

    def add_on(j):
        arrived(t_r.at[halves(j)], rt_r.at[j])
        spots = slice(STARTS[j], STARTS[j] + SIZES[j] // 2)
        part[3, spots, :, :CA] = (
            part[3, spots, :, :CA].astype(jnp.float32) + t_r[STARTS[j] // 2 : STARTS[j + 1] // 2].astype(jnp.float32)
        ).astype(jnp.bfloat16)
        put(part.at[3, first(j), :, wide], g_l.at[first(j)], send.at[11], rg_l.at[j], along(1))
        arrived(t_l.at[halves(j)], rt_l.at[j])
        spots = slice(STARTS[j] + SIZES[j] // 2, STARTS[j + 1])
        part[1, spots, :, :CA] = (
            part[1, spots, :, :CA].astype(jnp.float32) + t_l[STARTS[j] // 2 : STARTS[j + 1] // 2].astype(jnp.float32)
        ).astype(jnp.bfloat16)
        put(part.at[1, second(j), :, wide], g_r.at[second(j)], send.at[12], rg_r.at[j], along(3))

    def finish(j):
        arrived(g_l.at[chunk(j)], rg_l.at[j])
        arrived(g_r.at[chunk(j)], rg_r.at[j])
        spots = slice(STARTS[j], STARTS[j + 1])
        bias = row[:, :CA].reshape(1, 1, CA)
        e_out[spots] = (
            part[0, spots, :, :CA].astype(jnp.float32)
            + g_l[spots].astype(jnp.float32)
            + g_r[spots].astype(jnp.float32)
            + bias
        ).astype(jnp.bfloat16)
        for p in range(STARTS[j], STARTS[j + 1]):
            if p:
                put(e_out.at[p], ret_a.at[ORDER[p]], send.at[14], r_ra, source(ORDER[p]))
            else:
                ret_a[0] = e_out[0]

    def blocks_b(j):
        slots_b[0] = gathered(0, normed[:, CA:])
        total = info[0, 4:5, :]
        for k in range(1, 4):
            arrived(info.at[k], r_info.at[k - 1])
            arrived(norm_b.at[k], r_nb.at[k - 1])
            slots_b[k] = gathered(k, norm_b[k])
            total = total + info[k, 4:5, :]
        cnt_out[...] = total

    def send_b(j):
        for p in range(1, PEERS):
            n = ORDER[p]
            put(
                slots_b.at[:, n],
                x_in.at[:, p, :, pl.ds(CA, CB)],
                send.at[3],
                r_b.at[CHUNK_OF[p]],
                plane(n),
            )
            put(cnt_out, cnt_in.at[n], send.at[4], r_cnt, plane(n))
        x_in[:, 0, :, CA:] = slots_b[:, 0]

    def weights(j):
        for copy in loads[7:]:
            copy.wait()

    steps = {
        "gath": blocks_b,
        "send": send_b,
        "wts": weights,
        "own": own,
        "fwd": forward,
        "ready": ready,
        "up": project_up,
        "down": project_down,
        "give": give_back,
        "add": add_on,
        "fin": finish,
    }
    for entry in SCHEDULE.split():
        with jax.named_scope(entry):
            steps[entry[:-1]](int(entry[-1]))

    with jax.named_scope("load"):
        arrived(cnt_in.at[pl.ds(1, PEERS - 1)], r_cnt)
        cnt_in[0] = cnt_out[...]
        load[...] = jnp.sum(cnt_in[...], axis=0)[:, :32]

    slot_cols = lax.broadcasted_iota(jnp.int32, (FRAMES, PEERS * CAP), 1)

    def combined(k, rows):
        table = jnp.concatenate([info[k], jnp.zeros((FRAMES - 8, FRAMES), jnp.int32)], axis=0)
        turned = jnp.transpose(table.astype(jnp.float32))
        code0, code1 = turned[:, 2:3], turned[:, 3:4]
        weight0 = code0 / (code0 + code1)
        weight1 = code1 / (code0 + code1)
        spots = turned.astype(jnp.int32)
        pick0 = (slot_cols == spots[:, 0:1]).astype(jnp.float32).astype(jnp.bfloat16)
        pick1 = (slot_cols == spots[:, 1:2]).astype(jnp.float32).astype(jnp.bfloat16)
        out0 = jnp.dot(pick0, rows, preferred_element_type=jnp.float32)
        out1 = jnp.dot(pick1, rows, preferred_element_type=jnp.float32)
        return out0 * weight0 + out1 * weight1

    with jax.named_scope("blocks"):
        with jax.named_scope("wait_rb"):
            arrived(ret_b.at[:, pl.ds(1, PEERS - 1)], r_rb)
        for k in range(1, 4):
            y_out[k - 1] = combined(k, ret_b[k].reshape(PEERS * CAP, CB)).astype(jnp.bfloat16)
            put(y_out.at[k - 1], y_in.at[k - 1], send.at[15], r_y.at[k - 1], along(4 - k))
    with jax.named_scope("own_rows"):
        own_b = combined(0, ret_b[0].reshape(PEERS * CAP, CB))
        with jax.named_scope("wait_ra"):
            arrived(ret_a.at[pl.ds(1, PEERS - 1)], r_ra)
        own_a = combined(0, ret_a[...].reshape(PEERS * CAP, CA))
    with jax.named_scope("mix"):
        mixed[:, :CA] = (frames[:, :CA].astype(jnp.float32) + own_a).astype(jnp.bfloat16)
        for k in range(1, 4):
            arrived(y_in.at[k - 1], r_y.at[k - 1])
            own_b = own_b + y_in[k - 1].astype(jnp.float32)
        mixed[:, CA:] = (frames[:, CA:].astype(jnp.float32) + own_b).astype(jnp.bfloat16)

    with jax.named_scope("sent"):
        rest = pl.ds(1, PEERS - 1)
        some = pl.ds(1, 3)
        half = pl.ds(0, PEERS // 2)
        arrived(info.at[some], send.at[0])
        arrived(norm_b.at[some], send.at[1])
        arrived(slots_a.at[rest], send.at[2])
        arrived(slots_b.at[:, rest], send.at[3])
        arrived(cnt_in.at[rest], send.at[4])
        arrived(e_out, send.at[5])
        arrived(e_out, send.at[6])
        arrived(e_out.at[half], send.at[7])
        arrived(e_out.at[half], send.at[8])
        arrived(e_out.at[half], send.at[9])
        arrived(e_out.at[half], send.at[10])
        arrived(e_out, send.at[11])
        arrived(e_out, send.at[12])
        arrived(slots_b.at[:, rest], send.at[13])
        arrived(slots_a.at[rest], send.at[14])
        arrived(y_out, send.at[15])


def per_device(frames, gain, nbias, routes, codes, limits, up_w, up_b, down_w, down_b):
    vmem = pl.BlockSpec(memory_space=pltpu.VMEM)
    hbm = pl.BlockSpec(memory_space=pltpu.HBM)
    bf16, f32, i32 = jnp.bfloat16, jnp.float32, jnp.int32
    dma = pltpu.SemaphoreType.DMA
    mixed, load = pl.pallas_call(
        kernel,
        out_shape=(
            jax.ShapeDtypeStruct((FRAMES, D), bf16),
            jax.ShapeDtypeStruct((1, 32), i32),
        ),
        in_specs=[hbm] * 10,
        out_specs=(vmem, vmem),
        scratch_shapes=[
            pltpu.VMEM((FRAMES, D), bf16),
            pltpu.VMEM((1, D), f32),
            pltpu.VMEM((1, D), f32),
            pltpu.VMEM((2, FRAMES), i32),
            pltpu.VMEM((2, FRAMES), i32),
            pltpu.SMEM((32,), i32),
            pltpu.VMEM((1, D), f32),
            pltpu.VMEM((8, D), f32),
            pltpu.VMEM((D, D), bf16),
            pltpu.VMEM((D, D), bf16),
            pltpu.VMEM((PEERS, CAP, CA), bf16),
            pltpu.VMEM((4, FRAMES, CB), bf16),
            pltpu.VMEM((4, PEERS, CAP, CB), bf16),
            pltpu.VMEM((4, PEERS, CAP, D), bf16),
            pltpu.VMEM((4 * max(SIZES) * CAP, D), bf16),
            pltpu.VMEM((4, PEERS, CAP, D), bf16),
            pltpu.VMEM((PEERS // 2, CAP, CA), bf16),
            pltpu.VMEM((PEERS // 2, CAP, CA), bf16),
            pltpu.VMEM((PEERS, CAP, CA), bf16),
            pltpu.VMEM((PEERS, CAP, CA), bf16),
            pltpu.VMEM((PEERS, CAP, CA), bf16),
            pltpu.VMEM((PEERS, CAP, CA), bf16),
            pltpu.VMEM((4, PEERS, CAP, CB), bf16),
            pltpu.VMEM((3, FRAMES, CB), bf16),
            pltpu.VMEM((3, FRAMES, CB), bf16),
            pltpu.VMEM((4, 8, FRAMES), i32),
            pltpu.VMEM((1, FRAMES), i32),
            pltpu.VMEM((PEERS, 1, FRAMES), i32),
            pltpu.VMEM((1, D), f32),
            dma((10,)),
            dma((16,)),
            dma((CHUNKS,)),
            dma((CHUNKS,)),
            dma((3,)),
            dma((3,)),
            dma((CHUNKS,)),
            dma((CHUNKS,)),
            dma((CHUNKS,)),
            dma((CHUNKS,)),
            dma((CHUNKS,)),
            dma((CHUNKS,)),
            dma((CHUNKS,)),
            dma((CHUNKS,)),
            dma,
            dma,
            dma((3,)),
            dma,
        ],
        compiler_params=pltpu.CompilerParams(
            collective_id=0, has_side_effects=True, vmem_limit_bytes=30 << 20
        ),
        name="moe",
    )(
        *[
            pltpu.with_memory_space_constraint(value, pltpu.HBM)
            for value in (
                frames,
                gain.reshape(1, D),
                nbias.reshape(1, D),
                routes.T,
                codes.T,
                limits,
                up_w,
                up_b,
                down_w,
                down_b,
            )
        ],
    )
    return mixed, load.reshape(32)


def solution(mesh):
    both = ("dp", "expert")
    in_specs = (
        P(both, None),
        P(),
        P(),
        P(both, None),
        P(both, None),
        P(),
        P(both, None, None),
        P(both, None),
        P(both, None, None),
        P(),
    )
    out_specs = (P(both, None), P())
    return jax.shard_map(
        per_device, mesh=mesh, in_specs=in_specs, out_specs=out_specs, check_vma=False
    )
```

time: 83.9 us -> 67 us (0.80)
  Pallas kernels: 80.3 us -> 65 us
  local copies, waits for them, and re-layouts: 2.8 us -> 1.22 us
    pallas_call x1, Pallas kernels: 80.3 us -> 65 us  [per_device(): pl.pallas_call(kernel, out_shape=(jax.ShapeDtypeStruct((FRAMES, D), bf16)...]
    unnamed x2, local copies, waits for them, and re-layouts: 2.8 us -> 1.22 us
where the time goes in v2:
time: 67 us; the launch traced here: 66.9 us
  Pallas kernels  65 us (97%)
  local copies, waits for them, and re-layouts  1.22 us (2%)
    pallas_call x1, Pallas kernels, per_device(): pl.pallas_call(kernel, out_shape=(jax.ShapeDtypeStruct((FRAMES, D), bf16)...  65 us

profile of v2, /device:TPU:0, one launch (start us, length us, event | category | flops | bytes accessed | tf_op | source)
XLA Modules:
  0.0 66.9 jit_solution(13109605094846009644)
XLA Ops:
  0.6 65.0 %moe.1 = (bf16[128,1024]{1,0:T(8,128)(2,1)S(1)}, s32[1,32]{1,0:T(1,128)S(1)}) custom-call(bf16[128,1024]{1,0:T(8,128)(2,1)} %frames_hbm.1, f32[1,1024]{1,0:T(1,128)} %bitcast.6, f32[1,1024]{1,0:T(1,128)} %bitcast.7, s32[2,128]{1,0:T(2,128)} %bitcast.8, s32[2,128]{1,0:T(2,128)} %bitcast.9, s32[32]{0:T(128)} %limits_hbm.1, bf16[1,1024,1024]{2,1,0:T(8,128)(2,1)} %up_hbm.1, ...), custom_call_target="tpu_custom_call" | custom-call | tf_op jit(solution)/shard_map/moe/pallas_call | solution.py:484
  65.7 0.7 %copy.14 = bf16[128,1024]{1,0:T(8,128)(2,1)} copy(bf16[128,1024]{1,0:T(8,128)(2,1)S(1)} %get-tuple-element.8) | data formatting | bytes 524288
  66.4 0.5 copy.15

commit v3 on v2

--- a/solution.py
+++ b/solution.py
@@ -1,5 +1,3 @@
-import random
-
 import jax
 import jax.numpy as jnp
 from jax import lax
@@ -15,6 +13,8 @@
 PEERS = 32
 CB = 384
 CA = D - CB
+RB = 384
+RA = D - RB
 SIZES = [8, 8, 8, 8]
 CHUNKS = len(SIZES)
 STARTS = [sum(SIZES[:j]) for j in range(CHUNKS + 1)]
@@ -22,19 +22,21 @@
 TILE = 256
 
 
-def plane_order():
-    rest = list(range(1, PEERS))
-    random.Random(5).shuffle(rest)
-    return [0] + rest
-
-
-ORDER = plane_order()
-SCHEDULE = (
-    "own0 gath0 send0 own1 fwd0 own2 fwd1 own3 wts0 "
-    "ready0 up0 fwd2 down0 give0 ready1 up1 fwd3 down1 give1 add0 "
-    "ready2 up2 down2 give2 add1 ready3 up3 down3 give3 fin0 add2 fin1 add3 fin2 fin3"
-)
 OFFSETS = [((n // 2) % 4, n // 8, n % 2) for n in range(PEERS)]
+
+
+ORDER = [
+    0, 6, 8, 30, 14, 26, 2, 18, 15, 13, 1, 27, 17, 31, 28, 10,
+    21, 25, 4, 19, 23, 16, 12, 5, 7, 9, 3, 29, 11, 22, 20, 24,
+]
+SCHEDULE = [
+    "sa0", "sa1", "sa2", "sa3", "own0", "gath0", "sb0", "sb1",
+    "sb2", "sb3", "cnt0", "own1", "fwd0", "own2", "fwd1", "own3",
+    "wts0", "ready0", "up0", "fwd2", "down0", "give0", "ready1", "up1",
+    "fwd3", "down1", "give1", "ready2", "up2", "add0", "down2", "give2",
+    "ready3", "up3", "add1", "down3", "give3", "add2", "fin0", "fin1",
+    "add3", "fin2", "fin3",
+]
 
 
 def kernel(
@@ -130,11 +132,6 @@
         pltpu.make_async_copy(ref, ref, sem).wait()
 
     with jax.named_scope("greet"):
-        barrier = pltpu.get_barrier_semaphore()
-        for n in range(1, PEERS):
-            pl.semaphore_signal(barrier, inc=1, device_id=plane(n), device_id_type=MESH)
-        for k in range(1, 4):
-            pl.semaphore_signal(barrier, inc=1, device_id=along(k), device_id_type=MESH)
         loads = [
             pltpu.make_async_copy(src, dst, w_sem.at[i])
             for i, (src, dst) in enumerate(
@@ -154,16 +151,13 @@
         ]
         for copy in loads:
             copy.start()
-        for copy in loads[:6]:
+        barrier = pltpu.get_barrier_semaphore()
+        for n in range(1, PEERS):
+            pl.semaphore_signal(barrier, inc=1, device_id=plane(n), device_id_type=MESH)
+        for k in range(1, 4):
+            pl.semaphore_signal(barrier, inc=1, device_id=along(k), device_id_type=MESH)
+        for copy in loads[3:6]:
             copy.wait()
-
-    with jax.named_scope("norm"):
-        values = frames[...].astype(jnp.float32)
-        center = jnp.mean(values, axis=-1, keepdims=True)
-        shifted = values - center
-        spread = jnp.mean(shifted * shifted, axis=-1, keepdims=True)
-        normed = (shifted * lax.rsqrt(spread + EPS) * gain[...] + nbias[...]).astype(jnp.bfloat16)
-        norm_b[0] = normed[:, CA:]
 
     with jax.named_scope("route"):
         chosen = routes[...]
@@ -202,6 +196,16 @@
         info[0, 2:4, :] = codes[...]
         info[0, 4:8, :] = counts[0:4, :]
 
+    with jax.named_scope("norm"):
+        for copy in loads[:3]:
+            copy.wait()
+        values = frames[...].astype(jnp.float32)
+        center = jnp.mean(values, axis=-1, keepdims=True)
+        shifted = values - center
+        spread = jnp.mean(shifted * shifted, axis=-1, keepdims=True)
+        normed = (shifted * lax.rsqrt(spread + EPS) * gain[...] + nbias[...]).astype(jnp.bfloat16)
+        norm_b[0] = normed[:, CA:]
+
     slot_ids = lax.broadcasted_iota(jnp.int32, (PEERS * CAP, FRAMES), 0)
 
     def gathered(k, rows):
@@ -222,7 +226,7 @@
         loads[6].wait()
         row = down_b[pl.ds(lax.rem(mine, 8), 1), :]
         lane = lax.broadcasted_iota(jnp.int32, (1, D), 1)
-        brow[...] = jnp.where(lane >= CA, row * 0.25, 0.0)
+        brow[...] = jnp.where(lane >= RA, row * 0.25, 0.0)
 
     with jax.named_scope("met"):
         pl.semaphore_wait(barrier, PEERS - 1 + 3)
@@ -230,15 +234,6 @@
         for k in range(1, 4):
             put(info.at[0], info.at[k], send.at[0], r_info.at[k - 1], along(k))
             put(norm_b.at[0], norm_b.at[k], send.at[1], r_nb.at[k - 1], along(k))
-        for p in range(1, PEERS):
-            n = ORDER[p]
-            put(
-                slots_a.at[n],
-                x_in.at[0, p, :, pl.ds(0, CA)],
-                send.at[2],
-                r_a.at[CHUNK_OF[p]],
-                plane(n),
-            )
         x_in[0, 0, :, :CA] = slots_a[0]
 
     def chunk(j):
@@ -259,6 +254,8 @@
 
     wide = pl.ds(0, CA)
     narrow = pl.ds(CA, CB)
+    wide_back = pl.ds(0, RA)
+    narrow_back = pl.ds(RA, RB)
 
     def own(j):
         arrived(x_in.at[0, remote(j), :, wide], r_a.at[j])
@@ -325,43 +322,43 @@
         lax.fori_loop(0, D // TILE, step, 0)
 
     def give_back(j):
-        put(part.at[2, first(j), :, wide], t_r.at[halves(j)], send.at[9], rt_r.at[j], along(1))
-        put(part.at[2, second(j), :, wide], t_l.at[halves(j)], send.at[10], rt_l.at[j], along(3))
-        put(part.at[3, second(j), :, wide], g_l.at[second(j)], send.at[11], rg_l.at[j], along(1))
-        put(part.at[1, first(j), :, wide], g_r.at[first(j)], send.at[12], rg_r.at[j], along(3))
+        put(part.at[2, first(j), :, wide_back], t_r.at[halves(j)], send.at[9], rt_r.at[j], along(1))
+        put(part.at[2, second(j), :, wide_back], t_l.at[halves(j)], send.at[10], rt_l.at[j], along(3))
+        put(part.at[3, second(j), :, wide_back], g_l.at[second(j)], send.at[11], rg_l.at[j], along(1))
+        put(part.at[1, first(j), :, wide_back], g_r.at[first(j)], send.at[12], rg_r.at[j], along(3))
         for p in range(STARTS[j], STARTS[j + 1]):
             if p:
                 put(
-                    part.at[:, p, :, narrow],
+                    part.at[:, p, :, narrow_back],
                     ret_b.at[:, ORDER[p]],
                     send.at[13],
                     r_rb,
                     source(ORDER[p]),
                 )
             else:
-                ret_b[:, 0] = part[:, 0, :, CA:]
+                ret_b[:, 0] = part[:, 0, :, RA:]
 
     def add_on(j):
         arrived(t_r.at[halves(j)], rt_r.at[j])
         spots = slice(STARTS[j], STARTS[j] + SIZES[j] // 2)
-        part[3, spots, :, :CA] = (
-            part[3, spots, :, :CA].astype(jnp.float32) + t_r[STARTS[j] // 2 : STARTS[j + 1] // 2].astype(jnp.float32)
+        part[3, spots, :, :RA] = (
+            part[3, spots, :, :RA].astype(jnp.float32) + t_r[STARTS[j] // 2 : STARTS[j + 1] // 2].astype(jnp.float32)
         ).astype(jnp.bfloat16)
-        put(part.at[3, first(j), :, wide], g_l.at[first(j)], send.at[11], rg_l.at[j], along(1))
+        put(part.at[3, first(j), :, wide_back], g_l.at[first(j)], send.at[11], rg_l.at[j], along(1))
         arrived(t_l.at[halves(j)], rt_l.at[j])
         spots = slice(STARTS[j] + SIZES[j] // 2, STARTS[j + 1])
-        part[1, spots, :, :CA] = (
-            part[1, spots, :, :CA].astype(jnp.float32) + t_l[STARTS[j] // 2 : STARTS[j + 1] // 2].astype(jnp.float32)
+        part[1, spots, :, :RA] = (
+            part[1, spots, :, :RA].astype(jnp.float32) + t_l[STARTS[j] // 2 : STARTS[j + 1] // 2].astype(jnp.float32)
         ).astype(jnp.bfloat16)
-        put(part.at[1, second(j), :, wide], g_r.at[second(j)], send.at[12], rg_r.at[j], along(3))
+        put(part.at[1, second(j), :, wide_back], g_r.at[second(j)], send.at[12], rg_r.at[j], along(3))
 
     def finish(j):
         arrived(g_l.at[chunk(j)], rg_l.at[j])
         arrived(g_r.at[chunk(j)], rg_r.at[j])
         spots = slice(STARTS[j], STARTS[j + 1])
-        bias = row[:, :CA].reshape(1, 1, CA)
+        bias = row[:, :RA].reshape(1, 1, RA)
         e_out[spots] = (
-            part[0, spots, :, :CA].astype(jnp.float32)
+            part[0, spots, :, :RA].astype(jnp.float32)
             + g_l[spots].astype(jnp.float32)
             + g_r[spots].astype(jnp.float32)
             + bias
@@ -381,19 +378,33 @@
             slots_b[k] = gathered(k, norm_b[k])
             total = total + info[k, 4:5, :]
         cnt_out[...] = total
+        x_in[:, 0, :, CA:] = slots_b[:, 0]
+
+    def send_a(j):
+        for p in range(max(STARTS[j], 1), STARTS[j + 1]):
+            n = ORDER[p]
+            put(
+                slots_a.at[n],
+                x_in.at[0, p, :, pl.ds(0, CA)],
+                send.at[2],
+                r_a.at[j],
+                plane(n),
+            )
 
     def send_b(j):
-        for p in range(1, PEERS):
+        for p in range(max(STARTS[j], 1), STARTS[j + 1]):
             n = ORDER[p]
             put(
                 slots_b.at[:, n],
                 x_in.at[:, p, :, pl.ds(CA, CB)],
                 send.at[3],
-                r_b.at[CHUNK_OF[p]],
+                r_b.at[j],
                 plane(n),
             )
+
+    def send_counts(j):
+        for n in range(1, PEERS):
             put(cnt_out, cnt_in.at[n], send.at[4], r_cnt, plane(n))
-        x_in[:, 0, :, CA:] = slots_b[:, 0]
 
     def weights(j):
         for copy in loads[7:]:
@@ -401,7 +412,9 @@
 
     steps = {
         "gath": blocks_b,
-        "send": send_b,
+        "sa": send_a,
+        "sb": send_b,
+        "cnt": send_counts,
         "wts": weights,
         "own": own,
         "fwd": forward,
@@ -412,7 +425,7 @@
         "add": add_on,
         "fin": finish,
     }
-    for entry in SCHEDULE.split():
+    for entry in SCHEDULE:
         with jax.named_scope(entry):
             steps[entry[:-1]](int(entry[-1]))
 
@@ -423,7 +436,7 @@
 
     slot_cols = lax.broadcasted_iota(jnp.int32, (FRAMES, PEERS * CAP), 1)
 
-    def combined(k, rows):
+    def picks(k):
         table = jnp.concatenate([info[k], jnp.zeros((FRAMES - 8, FRAMES), jnp.int32)], axis=0)
         turned = jnp.transpose(table.astype(jnp.float32))
         code0, code1 = turned[:, 2:3], turned[:, 3:4]
@@ -432,6 +445,10 @@
         spots = turned.astype(jnp.int32)
         pick0 = (slot_cols == spots[:, 0:1]).astype(jnp.float32).astype(jnp.bfloat16)
         pick1 = (slot_cols == spots[:, 1:2]).astype(jnp.float32).astype(jnp.bfloat16)
+        return pick0, pick1, weight0, weight1
+
+    def weighted(found, rows):
+        pick0, pick1, weight0, weight1 = found
         out0 = jnp.dot(pick0, rows, preferred_element_type=jnp.float32)
         out1 = jnp.dot(pick1, rows, preferred_element_type=jnp.float32)
         return out0 * weight0 + out1 * weight1
@@ -440,19 +457,20 @@
         with jax.named_scope("wait_rb"):
             arrived(ret_b.at[:, pl.ds(1, PEERS - 1)], r_rb)
         for k in range(1, 4):
-            y_out[k - 1] = combined(k, ret_b[k].reshape(PEERS * CAP, CB)).astype(jnp.bfloat16)
+            y_out[k - 1] = weighted(picks(k), ret_b[k].reshape(PEERS * CAP, RB)).astype(jnp.bfloat16)
             put(y_out.at[k - 1], y_in.at[k - 1], send.at[15], r_y.at[k - 1], along(4 - k))
     with jax.named_scope("own_rows"):
-        own_b = combined(0, ret_b[0].reshape(PEERS * CAP, CB))
+        mine_at = picks(0)
+        own_b = weighted(mine_at, ret_b[0].reshape(PEERS * CAP, RB))
         with jax.named_scope("wait_ra"):
             arrived(ret_a.at[pl.ds(1, PEERS - 1)], r_ra)
-        own_a = combined(0, ret_a[...].reshape(PEERS * CAP, CA))
+        own_a = weighted(mine_at, ret_a[...].reshape(PEERS * CAP, RA))
     with jax.named_scope("mix"):
-        mixed[:, :CA] = (frames[:, :CA].astype(jnp.float32) + own_a).astype(jnp.bfloat16)
+        mixed[:, :RA] = (frames[:, :RA].astype(jnp.float32) + own_a).astype(jnp.bfloat16)
         for k in range(1, 4):
             arrived(y_in.at[k - 1], r_y.at[k - 1])
             own_b = own_b + y_in[k - 1].astype(jnp.float32)
-        mixed[:, CA:] = (frames[:, CA:].astype(jnp.float32) + own_b).astype(jnp.bfloat16)
+        mixed[:, RA:] = (frames[:, RA:].astype(jnp.float32) + own_b).astype(jnp.bfloat16)
 
     with jax.named_scope("sent"):
         rest = pl.ds(1, PEERS - 1)
@@ -463,17 +481,28 @@
         arrived(slots_a.at[rest], send.at[2])
         arrived(slots_b.at[:, rest], send.at[3])
         arrived(cnt_in.at[rest], send.at[4])
-        arrived(e_out, send.at[5])
-        arrived(e_out, send.at[6])
-        arrived(e_out.at[half], send.at[7])
-        arrived(e_out.at[half], send.at[8])
+        arrived(x_in.at[0, :, :, wide], send.at[5])
+        arrived(x_in.at[0, :, :, wide], send.at[6])
+        arrived(x_in.at[0, half, :, wide], send.at[7])
+        arrived(x_in.at[0, half, :, wide], send.at[8])
         arrived(e_out.at[half], send.at[9])
         arrived(e_out.at[half], send.at[10])
         arrived(e_out, send.at[11])
         arrived(e_out, send.at[12])
-        arrived(slots_b.at[:, rest], send.at[13])
-        arrived(slots_a.at[rest], send.at[14])
+        arrived(ret_b.at[:, rest], send.at[13])
+        arrived(e_out.at[rest], send.at[14])
         arrived(y_out, send.at[15])
+
+
+def finish_kernel(mixed_in, load_in, mixed, load, sems):
+    copies = [
+        pltpu.make_async_copy(mixed_in, mixed, sems.at[0]),
+        pltpu.make_async_copy(load_in, load, sems.at[1]),
+    ]
+    for copy in copies:
+        copy.start()
+    for copy in copies:
+        copy.wait()
 
 
 def per_device(frames, gain, nbias, routes, codes, limits, up_w, up_b, down_w, down_b):
@@ -506,15 +535,15 @@
             pltpu.VMEM((4, PEERS, CAP, D), bf16),
             pltpu.VMEM((4 * max(SIZES) * CAP, D), bf16),
             pltpu.VMEM((4, PEERS, CAP, D), bf16),
-            pltpu.VMEM((PEERS // 2, CAP, CA), bf16),
-            pltpu.VMEM((PEERS // 2, CAP, CA), bf16),
-            pltpu.VMEM((PEERS, CAP, CA), bf16),
-            pltpu.VMEM((PEERS, CAP, CA), bf16),
-            pltpu.VMEM((PEERS, CAP, CA), bf16),
-            pltpu.VMEM((PEERS, CAP, CA), bf16),
-            pltpu.VMEM((4, PEERS, CAP, CB), bf16),
-            pltpu.VMEM((3, FRAMES, CB), bf16),
-            pltpu.VMEM((3, FRAMES, CB), bf16),
+            pltpu.VMEM((PEERS // 2, CAP, RA), bf16),
+            pltpu.VMEM((PEERS // 2, CAP, RA), bf16),
+            pltpu.VMEM((PEERS, CAP, RA), bf16),
+            pltpu.VMEM((PEERS, CAP, RA), bf16),
+            pltpu.VMEM((PEERS, CAP, RA), bf16),
+            pltpu.VMEM((PEERS, CAP, RA), bf16),
+            pltpu.VMEM((4, PEERS, CAP, RB), bf16),
+            pltpu.VMEM((3, FRAMES, RB), bf16),
+            pltpu.VMEM((3, FRAMES, RB), bf16),
             pltpu.VMEM((4, 8, FRAMES), i32),
             pltpu.VMEM((1, FRAMES), i32),
             pltpu.VMEM((PEERS, 1, FRAMES), i32),
@@ -559,6 +588,18 @@
             )
         ],
     )
+    mixed, load = pl.pallas_call(
+        finish_kernel,
+        out_shape=(
+            jax.ShapeDtypeStruct((FRAMES, D), bf16),
+            jax.ShapeDtypeStruct((1, 32), i32),
+        ),
+        in_specs=[vmem, vmem],
+        out_specs=(hbm, hbm),
+        scratch_shapes=[dma((2,))],
+        compiler_params=pltpu.CompilerParams(vmem_limit_bytes=1 << 20),
+        name="store",
+    )(mixed, load)
     return mixed, load.reshape(32)
 
 

time: 67 us -> 65.9 us (0.984)
  local copies, waits for them, and re-layouts: 1.22 us -> 0 us
    unnamed x2 -> x0, local copies, waits for them, and re-layouts: 1.22 us -> none
    pallas_call x1, Pallas kernels: 65 us -> 64.3 us  [per_device(): pl.pallas_call(kernel, out_shape=(jax.ShapeDtypeStruct((FRAMES, D), bf16)...]
    pallas_call x0 -> x1, Pallas kernels: none -> 0.72 us  [per_device(): pl.pallas_call(finish_kernel, out_shape=(jax.ShapeDtypeStruct((FRAMES, D)...]
where the time goes in v3:
time: 65.9 us; the launch traced here: 65.6 us
  Pallas kernels  65 us (99%)
    pallas_call x1, Pallas kernels, per_device(): pl.pallas_call(kernel, out_shape=(jax.ShapeDtypeStruct((FRAMES, D), bf16)...  64.3 us

profile of v3, /device:TPU:0, one launch (start us, length us, event | category | flops | bytes accessed | tf_op | source)
XLA Modules:
  0.0 65.6 jit_solution(14028623420631535984)
XLA Ops:
  0.6 64.3 %moe.1 = (bf16[128,1024]{1,0:T(8,128)(2,1)S(1)}, s32[1,32]{1,0:T(1,128)S(1)}) custom-call(bf16[128,1024]{1,0:T(8,128)(2,1)} %frames_hbm.1, f32[1,1024]{1,0:T(1,128)} %bitcast.5, f32[1,1024]{1,0:T(1,128)} %bitcast.6, s32[2,128]{1,0:T(2,128)} %bitcast.7, s32[2,128]{1,0:T(2,128)} %bitcast.8, s32[32]{0:T(128)} %limits_hbm.1, bf16[1,1024,1024]{2,1,0:T(8,128)(2,1)} %up_hbm.1, ...), custom_call_target="tpu_custom_call" | custom-call | tf_op jit(solution)/shard_map/moe/pallas_call | solution.py:513
  64.9 0.7 %store.1 = (bf16[128,1024]{1,0:T(8,128)(2,1)}, s32[1,32]{1,0:T(1,128)}) custom-call(bf16[128,1024]{1,0:T(8,128)(2,1)S(1)} %get-tuple-element.6.mixed_in, s32[1,32]{1,0:T(1,128)S(1)} %get-tuple-element.7.load_in), custom_call_target="tpu_custom_call" | custom-call | tf_op jit(solution)/shard_map/store/pallas_call | solution.py:591

commit v4 on v3

--- a/solution.py
+++ b/solution.py
@@ -17,6 +17,7 @@
 RA = D - RB
 SIZES = [8, 8, 8, 8]
 CHUNKS = len(SIZES)
+LOAD_SEM = [0, 0, 1, 2, 3, 3, 3, 4, 5, 5]
 STARTS = [sum(SIZES[:j]) for j in range(CHUNKS + 1)]
 CHUNK_OF = [j for j in range(CHUNKS) for _ in range(SIZES[j])]
 TILE = 256
@@ -26,16 +27,16 @@
 
 
 ORDER = [
-    0, 6, 8, 30, 14, 26, 2, 18, 15, 13, 1, 27, 17, 31, 28, 10,
-    21, 25, 4, 19, 23, 16, 12, 5, 7, 9, 3, 29, 11, 22, 20, 24,
+    0, 18, 30, 14, 26, 6, 8, 2, 15, 13, 1, 27, 17, 31, 28, 10,
+    21, 25, 4, 19, 23, 16, 12, 5, 20, 29, 22, 11, 7, 9, 3, 24,
 ]
 SCHEDULE = [
     "sa0", "sa1", "sa2", "sa3", "own0", "gath0", "sb0", "sb1",
     "sb2", "sb3", "cnt0", "own1", "fwd0", "own2", "fwd1", "own3",
     "wts0", "ready0", "up0", "fwd2", "down0", "give0", "ready1", "up1",
     "fwd3", "down1", "give1", "ready2", "up2", "add0", "down2", "give2",
-    "ready3", "up3", "add1", "down3", "give3", "add2", "fin0", "fin1",
-    "add3", "fin2", "fin3",
+    "ready3", "up3", "add1", "down3", "give3", "fin0", "add2", "fin1",
+    "add3", "fin2", "blk0", "fin3",
 ]
 
 
@@ -53,25 +54,19 @@
     mixed,
     load,
     frames,
-    gain,
-    nbias,
-    routes,
-    codes,
+    vectors,
+    pairs,
     limits,
-    up_b,
     down_b,
-    up,
-    down,
+    weights,
     slots_a,
     norm_b,
     slots_b,
     x_in,
     hid,
     part,
-    t_r,
-    t_l,
-    g_l,
-    g_r,
+    t,
+    g,
     e_out,
     ret_a,
     ret_b,
@@ -89,12 +84,9 @@
     r_nb,
     f_l,
     f_r,
-    h_l,
-    h_r,
-    rt_r,
-    rt_l,
-    rg_l,
-    rg_r,
+    r_h,
+    r_t,
+    r_g,
     r_ra,
     r_rb,
     r_y,
@@ -106,19 +98,17 @@
     z, c = lax.div(dp, 2), lax.rem(dp, 2)
     mine = dp * 4 + y
 
+    zs = [lax.rem(z + k, 4) * 2 for k in range(4)]
+    ys = [lax.rem(y + k, 4) * 4 + x for k in range(4)]
+    cs = [c, 1 - c]
+
     def plane(n):
         dy, dz, dc = OFFSETS[n]
-        return (
-            lax.rem(z + dz, 4) * 2 + lax.rem(c + dc, 2),
-            lax.rem(y + dy, 4) * 4 + x,
-        )
+        return (zs[dz] + cs[dc], ys[dy])
 
     def source(n):
         dy, dz, dc = OFFSETS[n]
-        return (
-            lax.rem(z + 4 - dz, 4) * 2 + lax.rem(c + 2 - dc, 2),
-            lax.rem(y + 4 - dy, 4) * 4 + x,
-        )
+        return (zs[-dz] + cs[dc], ys[-dy])
 
     def along(k):
         return (dp, y * 4 + lax.rem(x + k, 4))
@@ -133,19 +123,19 @@
 
     with jax.named_scope("greet"):
         loads = [
-            pltpu.make_async_copy(src, dst, w_sem.at[i])
+            pltpu.make_async_copy(src, dst, w_sem.at[LOAD_SEM[i]])
             for i, (src, dst) in enumerate(
                 [
+                    (routes_hbm, pairs.at[0]),
+                    (codes_hbm, pairs.at[1]),
+                    (limits_hbm, limits),
                     (frames_hbm, frames),
-                    (gain_hbm, gain),
-                    (nbias_hbm, nbias),
-                    (routes_hbm, routes),
-                    (codes_hbm, codes),
-                    (limits_hbm, limits),
+                    (gain_hbm, vectors.at[0]),
+                    (nbias_hbm, vectors.at[1]),
+                    (up_b_hbm, vectors.at[2]),
                     (down_b_hbm.at[pl.ds(pl.multiple_of(lax.div(mine, 8) * 8, 8), 8)], down_b),
-                    (up_b_hbm, up_b),
-                    (up_hbm.at[0], up),
-                    (down_hbm.at[0], down),
+                    (up_hbm.at[0], weights.at[0]),
+                    (down_hbm.at[0], weights.at[1]),
                 ]
             )
         ]
@@ -156,11 +146,11 @@
             pl.semaphore_signal(barrier, inc=1, device_id=plane(n), device_id_type=MESH)
         for k in range(1, 4):
             pl.semaphore_signal(barrier, inc=1, device_id=along(k), device_id_type=MESH)
-        for copy in loads[3:6]:
-            copy.wait()
+        arrived(pairs, w_sem.at[0])
+        loads[2].wait()
 
     with jax.named_scope("route"):
-        chosen = routes[...]
+        chosen = pairs[0]
         ids = lax.broadcasted_iota(jnp.int32, (FRAMES, FRAMES), 0)
         cols = lax.broadcasted_iota(jnp.int32, (FRAMES, FRAMES), 1)
         hit0 = (ids == chosen[0:1, :]).astype(jnp.float32)
@@ -193,17 +183,17 @@
             preferred_element_type=jnp.float32,
         ).astype(jnp.int32)
         info[0, 0:2, :] = spot
-        info[0, 2:4, :] = codes[...]
+        info[0, 2:4, :] = pairs[1]
         info[0, 4:8, :] = counts[0:4, :]
 
     with jax.named_scope("norm"):
-        for copy in loads[:3]:
-            copy.wait()
+        loads[3].wait()
+        arrived(vectors, w_sem.at[3])
         values = frames[...].astype(jnp.float32)
         center = jnp.mean(values, axis=-1, keepdims=True)
         shifted = values - center
         spread = jnp.mean(shifted * shifted, axis=-1, keepdims=True)
-        normed = (shifted * lax.rsqrt(spread + EPS) * gain[...] + nbias[...]).astype(jnp.bfloat16)
+        normed = (shifted * lax.rsqrt(spread + EPS) * vectors[0] + vectors[1]).astype(jnp.bfloat16)
         norm_b[0] = normed[:, CA:]
 
     slot_ids = lax.broadcasted_iota(jnp.int32, (PEERS * CAP, FRAMES), 0)
@@ -223,18 +213,18 @@
 
     with jax.named_scope("gather"):
         slots_a[...] = gathered(0, normed[:, :CA])
-        loads[6].wait()
+        loads[7].wait()
         row = down_b[pl.ds(lax.rem(mine, 8), 1), :]
         lane = lax.broadcasted_iota(jnp.int32, (1, D), 1)
         brow[...] = jnp.where(lane >= RA, row * 0.25, 0.0)
+        x_in[0, 0, :, :CA] = slots_a[0]
 
     with jax.named_scope("met"):
         pl.semaphore_wait(barrier, PEERS - 1 + 3)
     with jax.named_scope("send_a"):
         for k in range(1, 4):
-            put(info.at[0], info.at[k], send.at[0], r_info.at[k - 1], along(k))
+            put(info.at[0], info.at[k], send.at[0], r_info, along(k))
             put(norm_b.at[0], norm_b.at[k], send.at[1], r_nb.at[k - 1], along(k))
-        x_in[0, 0, :, :CA] = slots_a[0]
 
     def chunk(j):
         return pl.ds(STARTS[j], SIZES[j])
@@ -269,7 +259,7 @@
         put(
             x_in.at[0, chunk(j), :, wide],
             x_in.at[3, chunk(j), :, wide],
-            send.at[6],
+            send.at[5],
             f_r.at[j],
             along(3),
         )
@@ -279,30 +269,29 @@
         put(
             x_in.at[1, first(j), :, wide],
             x_in.at[2, first(j), :, wide],
-            send.at[7],
-            h_l.at[j],
+            send.at[5],
+            r_h.at[j],
             along(1),
         )
         arrived(x_in.at[3, chunk(j), :, wide], f_r.at[j])
         put(
             x_in.at[3, second(j), :, wide],
             x_in.at[2, second(j), :, wide],
-            send.at[8],
-            h_r.at[j],
+            send.at[5],
+            r_h.at[j],
             along(3),
         )
 
     def ready(j):
         arrived(x_in.at[:, remote(j), :, narrow], r_b.at[j])
-        arrived(x_in.at[2, first(j), :, wide], h_l.at[j])
-        arrived(x_in.at[2, second(j), :, wide], h_r.at[j])
+        arrived(x_in.at[2, chunk(j), :, wide], r_h.at[j])
 
     def project_up(j):
         def step(t, carry):
             lanes = pl.ds(pl.multiple_of(t * TILE, TILE), TILE)
             rows = x_in[:, STARTS[j] : STARTS[j + 1]].reshape(4 * SIZES[j] * CAP, D)
-            pre = jnp.dot(rows, up[:, lanes], preferred_element_type=jnp.float32)
-            pre = pre + up_b[:, lanes]
+            pre = jnp.dot(rows, weights[0, :, lanes], preferred_element_type=jnp.float32)
+            pre = pre + vectors[2, :, lanes]
             act = 0.5 * pre * (1.0 + lax.erf(pre * 0.7071067811865476))
             hid[: 4 * SIZES[j] * CAP, lanes] = act.astype(jnp.bfloat16)
             return carry
@@ -312,7 +301,7 @@
     def project_down(j):
         def step(t, carry):
             lanes = pl.ds(pl.multiple_of(t * TILE, TILE), TILE)
-            out = jnp.dot(hid[: 4 * SIZES[j] * CAP], down[:, lanes], preferred_element_type=jnp.float32)
+            out = jnp.dot(hid[: 4 * SIZES[j] * CAP], weights[1, :, lanes], preferred_element_type=jnp.float32)
             out = out + brow[:, lanes]
             part[:, STARTS[j] : STARTS[j + 1], :, lanes] = out.astype(jnp.bfloat16).reshape(
                 4, SIZES[j], CAP, TILE
@@ -322,16 +311,16 @@
         lax.fori_loop(0, D // TILE, step, 0)
 
     def give_back(j):
-        put(part.at[2, first(j), :, wide_back], t_r.at[halves(j)], send.at[9], rt_r.at[j], along(1))
-        put(part.at[2, second(j), :, wide_back], t_l.at[halves(j)], send.at[10], rt_l.at[j], along(3))
-        put(part.at[3, second(j), :, wide_back], g_l.at[second(j)], send.at[11], rg_l.at[j], along(1))
-        put(part.at[1, first(j), :, wide_back], g_r.at[first(j)], send.at[12], rg_r.at[j], along(3))
+        put(part.at[2, first(j), :, wide_back], t.at[0, halves(j)], send.at[6], r_t.at[j], along(1))
+        put(part.at[2, second(j), :, wide_back], t.at[1, halves(j)], send.at[6], r_t.at[j], along(3))
+        put(part.at[3, second(j), :, wide_back], g.at[0, second(j)], send.at[6], r_g.at[j], along(1))
+        put(part.at[1, first(j), :, wide_back], g.at[1, first(j)], send.at[6], r_g.at[j], along(3))
         for p in range(STARTS[j], STARTS[j + 1]):
             if p:
                 put(
                     part.at[:, p, :, narrow_back],
                     ret_b.at[:, ORDER[p]],
-                    send.at[13],
+                    send.at[7],
                     r_rb,
                     source(ORDER[p]),
                 )
@@ -339,41 +328,39 @@
                 ret_b[:, 0] = part[:, 0, :, RA:]
 
     def add_on(j):
-        arrived(t_r.at[halves(j)], rt_r.at[j])
+        arrived(t.at[:, halves(j)], r_t.at[j])
         spots = slice(STARTS[j], STARTS[j] + SIZES[j] // 2)
         part[3, spots, :, :RA] = (
-            part[3, spots, :, :RA].astype(jnp.float32) + t_r[STARTS[j] // 2 : STARTS[j + 1] // 2].astype(jnp.float32)
+            part[3, spots, :, :RA].astype(jnp.float32) + t[0, STARTS[j] // 2 : STARTS[j + 1] // 2].astype(jnp.float32)
         ).astype(jnp.bfloat16)
-        put(part.at[3, first(j), :, wide_back], g_l.at[first(j)], send.at[11], rg_l.at[j], along(1))
-        arrived(t_l.at[halves(j)], rt_l.at[j])
+        put(part.at[3, first(j), :, wide_back], g.at[0, first(j)], send.at[6], r_g.at[j], along(1))
         spots = slice(STARTS[j] + SIZES[j] // 2, STARTS[j + 1])
         part[1, spots, :, :RA] = (
-            part[1, spots, :, :RA].astype(jnp.float32) + t_l[STARTS[j] // 2 : STARTS[j + 1] // 2].astype(jnp.float32)
+            part[1, spots, :, :RA].astype(jnp.float32) + t[1, STARTS[j] // 2 : STARTS[j + 1] // 2].astype(jnp.float32)
         ).astype(jnp.bfloat16)
-        put(part.at[1, second(j), :, wide_back], g_r.at[second(j)], send.at[12], rg_r.at[j], along(3))
+        put(part.at[1, second(j), :, wide_back], g.at[1, second(j)], send.at[6], r_g.at[j], along(3))
 
     def finish(j):
-        arrived(g_l.at[chunk(j)], rg_l.at[j])
-        arrived(g_r.at[chunk(j)], rg_r.at[j])
+        arrived(g.at[:, chunk(j)], r_g.at[j])
         spots = slice(STARTS[j], STARTS[j + 1])
         bias = row[:, :RA].reshape(1, 1, RA)
         e_out[spots] = (
             part[0, spots, :, :RA].astype(jnp.float32)
-            + g_l[spots].astype(jnp.float32)
-            + g_r[spots].astype(jnp.float32)
+            + g[0, spots].astype(jnp.float32)
+            + g[1, spots].astype(jnp.float32)
             + bias
         ).astype(jnp.bfloat16)
         for p in range(STARTS[j], STARTS[j + 1]):
             if p:
-                put(e_out.at[p], ret_a.at[ORDER[p]], send.at[14], r_ra, source(ORDER[p]))
+                put(e_out.at[p], ret_a.at[ORDER[p]], send.at[8], r_ra, source(ORDER[p]))
             else:
                 ret_a[0] = e_out[0]
 
     def blocks_b(j):
         slots_b[0] = gathered(0, normed[:, CA:])
         total = info[0, 4:5, :]
+        arrived(info.at[pl.ds(1, 3)], r_info)
         for k in range(1, 4):
-            arrived(info.at[k], r_info.at[k - 1])
             arrived(norm_b.at[k], r_nb.at[k - 1])
             slots_b[k] = gathered(k, norm_b[k])
             total = total + info[k, 4:5, :]
@@ -406,33 +393,8 @@
         for n in range(1, PEERS):
             put(cnt_out, cnt_in.at[n], send.at[4], r_cnt, plane(n))
 
-    def weights(j):
-        for copy in loads[7:]:
-            copy.wait()
-
-    steps = {
-        "gath": blocks_b,
-        "sa": send_a,
-        "sb": send_b,
-        "cnt": send_counts,
-        "wts": weights,
-        "own": own,
-        "fwd": forward,
-        "ready": ready,
-        "up": project_up,
-        "down": project_down,
-        "give": give_back,
-        "add": add_on,
-        "fin": finish,
-    }
-    for entry in SCHEDULE:
-        with jax.named_scope(entry):
-            steps[entry[:-1]](int(entry[-1]))
-
-    with jax.named_scope("load"):
-        arrived(cnt_in.at[pl.ds(1, PEERS - 1)], r_cnt)
-        cnt_in[0] = cnt_out[...]
-        load[...] = jnp.sum(cnt_in[...], axis=0)[:, :32]
+    def weights_in(j):
+        arrived(weights, w_sem.at[5])
 
     slot_cols = lax.broadcasted_iota(jnp.int32, (FRAMES, PEERS * CAP), 1)
 
@@ -453,12 +415,38 @@
         out1 = jnp.dot(pick1, rows, preferred_element_type=jnp.float32)
         return out0 * weight0 + out1 * weight1
 
-    with jax.named_scope("blocks"):
+    def blocks_back(j):
         with jax.named_scope("wait_rb"):
             arrived(ret_b.at[:, pl.ds(1, PEERS - 1)], r_rb)
         for k in range(1, 4):
             y_out[k - 1] = weighted(picks(k), ret_b[k].reshape(PEERS * CAP, RB)).astype(jnp.bfloat16)
-            put(y_out.at[k - 1], y_in.at[k - 1], send.at[15], r_y.at[k - 1], along(4 - k))
+            put(y_out.at[k - 1], y_in.at[k - 1], send.at[9], r_y, along(4 - k))
+
+    steps = {
+        "gath": blocks_b,
+        "sa": send_a,
+        "sb": send_b,
+        "cnt": send_counts,
+        "wts": weights_in,
+        "own": own,
+        "fwd": forward,
+        "ready": ready,
+        "up": project_up,
+        "down": project_down,
+        "give": give_back,
+        "add": add_on,
+        "fin": finish,
+        "blk": blocks_back,
+    }
+    for entry in SCHEDULE:
+        with jax.named_scope(entry):
+            steps[entry[:-1]](int(entry[-1]))
+
+    with jax.named_scope("load"):
+        arrived(cnt_in.at[pl.ds(1, PEERS - 1)], r_cnt)
+        cnt_in[0] = cnt_out[...]
+        load[...] = jnp.sum(cnt_in[...], axis=0)[:, :32]
+
     with jax.named_scope("own_rows"):
         mine_at = picks(0)
         own_b = weighted(mine_at, ret_b[0].reshape(PEERS * CAP, RB))
@@ -467,31 +455,24 @@
         own_a = weighted(mine_at, ret_a[...].reshape(PEERS * CAP, RA))
     with jax.named_scope("mix"):
         mixed[:, :RA] = (frames[:, :RA].astype(jnp.float32) + own_a).astype(jnp.bfloat16)
+        arrived(y_in, r_y)
         for k in range(1, 4):
-            arrived(y_in.at[k - 1], r_y.at[k - 1])
             own_b = own_b + y_in[k - 1].astype(jnp.float32)
         mixed[:, RA:] = (frames[:, RA:].astype(jnp.float32) + own_b).astype(jnp.bfloat16)
 
     with jax.named_scope("sent"):
         rest = pl.ds(1, PEERS - 1)
-        some = pl.ds(1, 3)
-        half = pl.ds(0, PEERS // 2)
-        arrived(info.at[some], send.at[0])
-        arrived(norm_b.at[some], send.at[1])
+        three = pl.ds(0, 3)
+        arrived(info.at[pl.ds(1, 3)], send.at[0])
+        arrived(norm_b.at[pl.ds(1, 3)], send.at[1])
         arrived(slots_a.at[rest], send.at[2])
         arrived(slots_b.at[:, rest], send.at[3])
         arrived(cnt_in.at[rest], send.at[4])
-        arrived(x_in.at[0, :, :, wide], send.at[5])
-        arrived(x_in.at[0, :, :, wide], send.at[6])
-        arrived(x_in.at[0, half, :, wide], send.at[7])
-        arrived(x_in.at[0, half, :, wide], send.at[8])
-        arrived(e_out.at[half], send.at[9])
-        arrived(e_out.at[half], send.at[10])
-        arrived(e_out, send.at[11])
-        arrived(e_out, send.at[12])
-        arrived(ret_b.at[:, rest], send.at[13])
-        arrived(e_out.at[rest], send.at[14])
-        arrived(y_out, send.at[15])
+        arrived(x_in.at[three, :, :, wide], send.at[5])
+        arrived(part.at[three, :, :, wide_back], send.at[6])
+        arrived(ret_b.at[:, rest], send.at[7])
+        arrived(e_out.at[rest], send.at[8])
+        arrived(y_out, send.at[9])
 
 
 def finish_kernel(mixed_in, load_in, mixed, load, sems):
@@ -520,25 +501,19 @@
         out_specs=(vmem, vmem),
         scratch_shapes=[
             pltpu.VMEM((FRAMES, D), bf16),
-            pltpu.VMEM((1, D), f32),
-            pltpu.VMEM((1, D), f32),
-            pltpu.VMEM((2, FRAMES), i32),
-            pltpu.VMEM((2, FRAMES), i32),
+            pltpu.VMEM((3, 1, D), f32),
+            pltpu.VMEM((2, 2, FRAMES), i32),
             pltpu.SMEM((32,), i32),
-            pltpu.VMEM((1, D), f32),
             pltpu.VMEM((8, D), f32),
-            pltpu.VMEM((D, D), bf16),
-            pltpu.VMEM((D, D), bf16),
+            pltpu.VMEM((2, D, D), bf16),
             pltpu.VMEM((PEERS, CAP, CA), bf16),
             pltpu.VMEM((4, FRAMES, CB), bf16),
             pltpu.VMEM((4, PEERS, CAP, CB), bf16),
             pltpu.VMEM((4, PEERS, CAP, D), bf16),
             pltpu.VMEM((4 * max(SIZES) * CAP, D), bf16),
             pltpu.VMEM((4, PEERS, CAP, D), bf16),
-            pltpu.VMEM((PEERS // 2, CAP, RA), bf16),
-            pltpu.VMEM((PEERS // 2, CAP, RA), bf16),
-            pltpu.VMEM((PEERS, CAP, RA), bf16),
-            pltpu.VMEM((PEERS, CAP, RA), bf16),
+            pltpu.VMEM((2, PEERS // 2, CAP, RA), bf16),
+            pltpu.VMEM((2, PEERS, CAP, RA), bf16),
             pltpu.VMEM((PEERS, CAP, RA), bf16),
             pltpu.VMEM((PEERS, CAP, RA), bf16),
             pltpu.VMEM((4, PEERS, CAP, RB), bf16),
@@ -548,15 +523,12 @@
             pltpu.VMEM((1, FRAMES), i32),
             pltpu.VMEM((PEERS, 1, FRAMES), i32),
             pltpu.VMEM((1, D), f32),
+            dma((6,)),
             dma((10,)),
-            dma((16,)),
-            dma((CHUNKS,)),
-            dma((CHUNKS,)),
+            dma((CHUNKS,)),
+            dma((CHUNKS,)),
+            dma,
             dma((3,)),
-            dma((3,)),
-            dma((CHUNKS,)),
-            dma((CHUNKS,)),
-            dma((CHUNKS,)),
             dma((CHUNKS,)),
             dma((CHUNKS,)),
             dma((CHUNKS,)),
@@ -564,7 +536,7 @@
             dma((CHUNKS,)),
             dma,
             dma,
-            dma((3,)),
+            dma,
             dma,
         ],
         compiler_params=pltpu.CompilerParams(

time: 65.9 us -> 65.4 us (level)
  Pallas kernels: 65 us -> 64.3 us
    pallas_call x1, Pallas kernels: 64.3 us -> 63.5 us  [per_device(): pl.pallas_call(kernel, out_shape=(jax.ShapeDtypeStruct((FRAMES, D), bf16)...]
where the time goes in v4:
time: 65.4 us; the launch traced here: 64.9 us
  Pallas kernels  64.3 us (98%)
    pallas_call x1, Pallas kernels, per_device(): pl.pallas_call(kernel, out_shape=(jax.ShapeDtypeStruct((FRAMES, D), bf16)...  63.5 us

profile of v4, /device:TPU:0, one launch (start us, length us, event | category | flops | bytes accessed | tf_op | source)
XLA Modules:
  0.0 64.9 jit_solution(4810981594282527243)
XLA Ops:
  0.6 63.5 %moe.1 = (bf16[128,1024]{1,0:T(8,128)(2,1)S(1)}, s32[1,32]{1,0:T(1,128)S(1)}) custom-call(bf16[128,1024]{1,0:T(8,128)(2,1)} %frames_hbm.1, f32[1,1024]{1,0:T(1,128)} %bitcast.5, f32[1,1024]{1,0:T(1,128)} %bitcast.6, s32[2,128]{1,0:T(2,128)} %bitcast.7, s32[2,128]{1,0:T(2,128)} %bitcast.8, s32[32]{0:T(128)} %limits_hbm.1, bf16[1,1024,1024]{2,1,0:T(8,128)(2,1)} %up_hbm.1, ...), custom_call_target="tpu_custom_call" | custom-call | tf_op jit(solution)/shard_map/moe/pallas_call | solution.py:494
  64.2 0.7 %store.1 = (bf16[128,1024]{1,0:T(8,128)(2,1)}, s32[1,32]{1,0:T(1,128)}) custom-call(bf16[128,1024]{1,0:T(8,128)(2,1)S(1)} %get-tuple-element.6.mixed_in, s32[1,32]{1,0:T(1,128)S(1)} %get-tuple-element.7.load_in), custom_call_target="tpu_custom_call" | custom-call | tf_op jit(solution)/shard_map/store/pallas_call | solution.py:563

commit v5 on v4

--- a/solution.py
+++ b/solution.py
@@ -32,8 +32,8 @@
 ]
 SCHEDULE = [
     "sa0", "sa1", "sa2", "sa3", "own0", "gath0", "sb0", "sb1",
-    "sb2", "sb3", "cnt0", "own1", "fwd0", "own2", "fwd1", "own3",
-    "wts0", "ready0", "up0", "fwd2", "down0", "give0", "ready1", "up1",
+    "sb2", "sb3", "own1", "fwd0", "own2", "fwd1", "own3", "wts0",
+    "ready0", "up0", "fwd2", "down0", "give0", "cnt0", "ready1", "up1",
     "fwd3", "down1", "give1", "ready2", "up2", "add0", "down2", "give2",
     "ready3", "up3", "add1", "down3", "give3", "fin0", "add2", "fin1",
     "add3", "fin2", "blk0", "fin3",

time: 65.4 us -> 65.7 us (level)
  no operation moved by 1% of the time
where the time goes in v5:
time: 65.7 us; the launch traced here: 64.9 us
  Pallas kernels  64.3 us (98%)
    pallas_call x1, Pallas kernels, per_device(): pl.pallas_call(kernel, out_shape=(jax.ShapeDtypeStruct((FRAMES, D), bf16)...  63.5 us

profile of v5, /device:TPU:0, one launch (start us, length us, event | category | flops | bytes accessed | tf_op | source)
XLA Modules:
  0.0 64.9 jit_solution(5270230591787335231)
XLA Ops:
  0.6 63.5 %moe.1 = (bf16[128,1024]{1,0:T(8,128)(2,1)S(1)}, s32[1,32]{1,0:T(1,128)S(1)}) custom-call(bf16[128,1024]{1,0:T(8,128)(2,1)} %frames_hbm.1, f32[1,1024]{1,0:T(1,128)} %bitcast.5, f32[1,1024]{1,0:T(1,128)} %bitcast.6, s32[2,128]{1,0:T(2,128)} %bitcast.7, s32[2,128]{1,0:T(2,128)} %bitcast.8, s32[32]{0:T(128)} %limits_hbm.1, bf16[1,1024,1024]{2,1,0:T(8,128)(2,1)} %up_hbm.1, ...), custom_call_target="tpu_custom_call" | custom-call | tf_op jit(solution)/shard_map/moe/pallas_call | solution.py:494
  64.2 0.7 %store.1 = (bf16[128,1024]{1,0:T(8,128)(2,1)}, s32[1,32]{1,0:T(1,128)}) custom-call(bf16[128,1024]{1,0:T(8,128)(2,1)S(1)} %get-tuple-element.6.mixed_in, s32[1,32]{1,0:T(1,128)S(1)} %get-tuple-element.7.load_in), custom_call_target="tpu_custom_call" | custom-call | tf_op jit(solution)/shard_map/store/pallas_call | solution.py:563
